TPU v7x, 16 devices: a 4x2x1 block of a 4x4x8 slice. The times are simulated.
16 devices in a mesh: rep: 4 (over y, z, core), dp: 4 (over x).
Axes of the slice: x: 4, y: 2, z: 1, core: 2. Of those that a mesh axis runs over, the one named last changes fastest.
The devices are a block of a 4x4x8 slice.
Arguments:
- x: bfloat16 [16, 4096, 768], P(('rep', 'dp')), parts along dimension 0
- dy: bfloat16 [16, 4096, 768], P(('rep', 'dp')), parts along dimension 0
- w_gate: bfloat16 [2, 768, 1792], replicated
- w_up: bfloat16 [2, 768, 1792], replicated
- w_down: bfloat16 [2, 1792, 768], replicated
- m_w_gate: float32 [2, 768, 1792], replicated
- m_w_up: float32 [2, 768, 1792], replicated
- m_w_down: float32 [2, 1792, 768], replicated
- v_w_gate: float32 [2, 768, 1792], replicated
- v_w_up: float32 [2, 768, 1792], replicated
- v_w_down: float32 [2, 1792, 768], replicated
Outputs:
- output 1: bfloat16 [8, 768, 1792], P('rep'), parts along dimension 0
- output 2: bfloat16 [8, 768, 1792], P('rep'), parts along dimension 0
- output 3: bfloat16 [8, 1792, 768], P('rep'), parts along dimension 0
- output 4: float32 [8, 768, 1792], P('rep'), parts along dimension 0
- output 5: float32 [8, 768, 1792], P('rep'), parts along dimension 0
- output 6: float32 [8, 1792, 768], P('rep'), parts along dimension 0
- output 7: float32 [8, 768, 1792], P('rep'), parts along dimension 0
- output 8: float32 [8, 768, 1792], P('rep'), parts along dimension 0
- output 9: float32 [8, 1792, 768], P('rep'), parts along dimension 0
There are 4 independent parts. A program takes and returns all parts, laid end to end along the dimension named above; an argument that names none is the same for every part.
All inputs are finite; a program needn't handle non-finite values.
Results may differ from a plain program's by a relative error of at most 0.022.
Values are sent between devices in bfloat16 or wider.
A program may use at most 768 MiB of HBM per device.

v0:
```python
import jax
import jax.numpy as jnp
from jax import lax
from jax.sharding import PartitionSpec as P

NAMES = ("w_gate", "w_up", "w_down")


def matmul(a, w):
    return jnp.dot(a, w, preferred_element_type=jnp.float32).astype(jnp.bfloat16)


def normed(h):
    wide = h.astype(jnp.float32)
    scale = lax.rsqrt(jnp.mean(wide**2, -1, keepdims=True) + 1e-6)
    return (wide * scale).astype(jnp.bfloat16)


def layer(h, w):
    a = normed(h)
    gate = jnp.dot(a, w["w_gate"], preferred_element_type=jnp.float32)
    up = jnp.dot(a, w["w_up"], preferred_element_type=jnp.float32)
    return h + matmul((jax.nn.silu(gate) * up).astype(jnp.bfloat16), w["w_down"])


def adamw(w, m, v, g):
    m = 0.9 * m + 0.1 * g
    v = 0.95 * v + 0.05 * g * g
    step = m * lax.rsqrt(v + 1e-8) + 0.1 * w
    return (w - 0.02 * step).astype(jnp.bfloat16), m, v


def clipped(gradients, sum_of_squares, count):
    factor = jnp.minimum(1.0, 0.5 * lax.rsqrt(sum_of_squares / count + 1e-30))
    return [g * factor for g in gradients]


def solution(mesh):
    def step(x, dy, *arrays):
        weights, m, v = (arrays[i : i + 3] for i in (0, 3, 6))
        layers = weights[0].shape[0]
        h, kept = x[0], []
        for number in range(layers):
            kept.append(h)
            h = layer(h, {name: w[number] for name, w in zip(NAMES, weights, strict=True)})
        by_h, summed = dy[0], [None] * layers
        for number in reversed(range(layers)):
            _, back = jax.vjp(lambda w, h: layer(h, w), {name: w[number] for name, w in zip(NAMES, weights, strict=True)}, kept[number])
            by_w, by_h = back(by_h)
            summed[number] = [lax.psum(by_w[name], "dp") for name in NAMES]
        gradients = [jnp.stack([summed[number][i] for number in range(layers)]).astype(jnp.float32) for i in range(3)]
        gradients = clipped(gradients, sum(jnp.sum(g * g) for g in gradients), sum(g.size for g in gradients))
        new = [adamw(w.astype(jnp.float32), m, v, g) for w, m, v, g in zip(weights, m, v, gradients, strict=True)]
        return tuple(one[which] for which in range(3) for one in new)

    return jax.shard_map(
        step,
        mesh=mesh,
        in_specs=(P(("rep", "dp"), None, None),) * 2 + (P(None, None, None),) * 9,
        out_specs=(P("rep", None, None),) * 9,
        check_vma=False,
    )
```

profile of v0, /device:TPU:112, one launch (start us, length us, event | category | flops | bytes accessed | tf_op | source)
XLA Modules:
  0.0 757.9 jit_solution(11019235134685696710)
XLA Ops:
  7.2 0.1 all-reduce.3.cloned.1.call-start
  7.3 8.6 %copy.20 = bf16[1,4096,768]{1,2,0:T(8,128)(2,1)} copy(bf16[1,4096,768]{2,1,0:T(8,128)(2,1)} %param.11) | data formatting | bytes 12582912 | tf_op args[0]
  15.9 4.1 fusion.18
  20.0 0.0 copy-start.5
  20.0 0.0 slice-start.2
  20.0 8.8 %copy.21 = bf16[1,4096,768]{1,2,0:T(8,128)(2,1)} copy(bf16[1,4096,768]{2,1,0:T(8,128)(2,1)} %param.12) | data formatting | bytes 12582912 | tf_op args[1]
  28.8 17.7 %convolution_convert_fusion.1 = bf16[4096,1792]{1,0:T(8,128)(2,1)} fusion(bf16[1,4096,768]{2,1,0:T(8,128)(2,1)} %param.12, bf16[2,1792,768]{2,1,0:T(8,128)(2,1)} %param.15), kind=kOutput, calls=%fused_computation.33 | convolution fusion | flops 11281629184 | bytes 23724032 | tf_op jit(solution)/shard_map/transpose(jvp())/dot_general | solution.py:10
  46.5 0.0 slice-done.2
  46.5 0.0 slice-done.3
  46.5 17.1 %fusion.103 = f32[4096,1792]{1,0:T(8,128)} fusion(bf16[2,768,1792]{2,1,0:T(8,128)(2,1)} %param.13, bf16[1,4096,768]{2,1,0:T(8,128)(2,1)S(1)} %bitcast.85, f32[4096]{0:T(1024)S(1)} %add_rsqrt_fusion), kind=kOutput, calls=%fused_computation.113 | convolution fusion | flops 11283726336 | bytes 38420480 | tf_op jit(solution)/shard_map/dot_general | solution.py:21
  63.5 0.0 copy-done.5
  63.6 33.1 %multiply_convert_fusion.1 = (bf16[4096,1792]{1,0:T(8,128)(2,1)}, f32[4096,1792]{1,0:T(8,128)}) fusion(f32[4096,1792]{1,0:T(8,128)} %fusion.103, bf16[2,768,1792]{2,1,0:T(8,128)(2,1)} %param.14, bf16[1,4096,768]{2,1,0:T(8,128)(2,1)} %param.11, f32[4096]{0:T(1024)S(1)} %add_rsqrt_fusion), kind=kOutput, calls=%fused_computation.17 | convolution fusion | flops 11327766528 | bytes 82460672 | tf_op jit(solution)/shard_map/dot_general | solution.py:22
  96.6 19.2 %fusion.22 = (f32[4096]{0:T(1024)S(1)}, bf16[4096,768]{0,1:T(8,128)(2,1)}) fusion(bf16[4096,1792]{1,0:T(8,128)(2,1)} %get-tuple-element.24, bf16[2,1792,768]{2,1,0:T(8,128)(2,1)} %param.15, bf16[1,4096,768]{1,2,0:T(8,128)(2,1)} %copy.20), kind=kOutput, calls=%fused_computation.55 | convolution fusion | flops 11290013696 | bytes 30031872 | tf_op jit(solution)/shard_map/dot_general | solution.py:10
  115.8 0.0 copy-start.3
  115.8 20.2 %fusion.55 = f32[4096,1792]{1,0:T(8,128)} fusion(bf16[4096,768]{0,1:T(8,128)(2,1)} %get-tuple-element.27, f32[4096]{0:T(1024)S(1)} %fusion.116, bf16[2,768,1792]{2,1,0:T(8,128)(2,1)} %param.14), kind=kOutput, calls=%fused_computation.90 | convolution fusion | flops 11283726336 | bytes 38420480 | tf_op jit(solution)/shard_map/jvp()/dot_general | solution.py:22
  136.0 0.0 copy-done.3
  136.0 39.8 %fusion.2 = (bf16[4096,1792]{1,0:T(8,128)(2,1)}, f32[4096,1792]{1,0:T(8,128)}) fusion(f32[4096,1792]{1,0:T(8,128)} %fusion.55, bf16[4096,1792]{1,0:T(8,128)(2,1)} %convolution_convert_fusion.1, bf16[2,768,1792]{2,1,0:T(8,128)(2,1)} %param.13, bf16[4096,768]{0,1:T(8,128)(2,1)} %get-tuple-element.27, f32[4096]{0:T(1024)S(1)} %fusion.116), kind=kOutput, calls=%fused_computation.8 | convolution fusion | flops 11371806720 | bytes 97140736 | tf_op jit(solution)/shard_map/jvp()/dot_general | solution.py:21
  175.8 26.0 %fusion.79 = bf16[1,1792,768]{2,1,0:T(8,128)(2,1)} fusion(bf16[1,4096,768]{2,1,0:T(8,128)(2,1)} %param.12, f32[4096,1792]{1,0:T(8,128)} %fusion.55, f32[4096,1792]{1,0:T(8,128)} %get-tuple-element.29), kind=kOutput, calls=%fused_computation.99 | convolution fusion | flops 11319705600 | bytes 67764224 | tf_op jit(solution)/shard_map/transpose(jvp())/dot_general | solution.py:10
  201.8 25.1 %fusion.76 = bf16[1,768,1792]{2,1,0:T(8,128)(2,1)} fusion(bf16[4096,1792]{1,0:T(8,128)(2,1)} %convolution_convert_fusion.1, bf16[4096,768]{0,1:T(8,128)(2,1)} %get-tuple-element.27, f32[4096]{0:T(1024)S(1)} %fusion.116, f32[4096,1792]{1,0:T(8,128)} %get-tuple-element.29), kind=kOutput, calls=%fused_computation.98 | convolution fusion | flops 11329142784 | bytes 53100544 | tf_op jit(solution)/shard_map/transpose(jvp())/dot_general | solution.py:22
  226.9 23.0 %fusion.43 = bf16[4096,768]{0,1:T(8,128)(2,1)} fusion(bf16[4096,1792]{1,0:T(8,128)(2,1)} %convolution_convert_fusion.1, bf16[2,768,1792]{2,1,0:T(8,128)(2,1)} %param.14, f32[4096,1792]{1,0:T(8,128)} %get-tuple-element.29), kind=kOutput, calls=%fused_computation.77 | convolution fusion | flops 11321475072 | bytes 53084160 | tf_op jit(solution)/shard_map/transpose(jvp())/dot_general | solution.py:22
  249.9 0.0 slice-start
  249.9 18.8 %fusion.82 = bf16[1,768,1792]{2,1,0:T(8,128)(2,1)} fusion(bf16[4096,1792]{1,0:T(8,128)(2,1)} %get-tuple-element.28, bf16[4096,768]{0,1:T(8,128)(2,1)} %get-tuple-element.27, f32[4096]{0:T(1024)S(1)} %fusion.116), kind=kOutput, calls=%fused_computation.100 | convolution fusion | flops 11283726336 | bytes 23740416 | tf_op jit(solution)/shard_map/transpose(jvp())/dot_general | solution.py:21
  268.7 0.0 copy-start.4
  268.7 0.0 slice-start.1
  268.7 20.6 %fusion.24 = (f32[4096]{0:T(1024)S(1)}, bf16[4096,768]{0,1:T(8,128)(2,1)}) fusion(bf16[4096,768]{0,1:T(8,128)(2,1)} %get-tuple-element.27, bf16[4096,768]{0,1:T(8,128)(2,1)} %fusion.43, bf16[4096,1792]{1,0:T(8,128)(2,1)} %get-tuple-element.28, bf16[2,768,1792]{2,1,0:T(8,128)(2,1)} %param.13), kind=kOutput, calls=%fused_computation.57 | convolution fusion | flops 11290013696 | bytes 36323328 | tf_op jit(solution)/shard_map/transpose(jvp())/dot_general | solution.py:21
  289.3 0.0 copy-done.4
  289.3 0.0 slice-done
  289.3 0.0 slice-done.1
  289.4 7.1 fusion.45
  296.5 0.0 copy-start.2
  296.5 2.7 copy-done.2
  299.2 16.2 %fusion.85 = bf16[1,1792,768]{2,1,0:T(8,128)(2,1)} fusion(bf16[4096,1792]{1,0:T(8,128)(2,1)} %get-tuple-element.24, bf16[4096,768]{0,1:T(8,128)(2,1)S(1)} %fusion.45), kind=kOutput, calls=%fused_computation.101 | convolution fusion | flops 11275665408 | bytes 23724032 | tf_op jit(solution)/shard_map/transpose(jvp())/dot_general | solution.py:10
  315.3 0.0 copy-start.6
  315.3 17.9 %convolution_convert_fusion = bf16[4096,1792]{1,0:T(8,128)(2,1)} fusion(bf16[4096,768]{0,1:T(8,128)(2,1)} %copy-done.2, bf16[2,1792,768]{2,1,0:T(8,128)(2,1)} %param.15), kind=kOutput, calls=%fused_computation.32 | convolution fusion | flops 11281629184 | bytes 23724032 | tf_op jit(solution)/shard_map/transpose(jvp())/dot_general | solution.py:10
  333.2 0.0 copy-done.6
  333.3 25.0 %fusion.86 = bf16[1,768,1792]{2,1,0:T(8,128)(2,1)} fusion(bf16[4096,1792]{1,0:T(8,128)(2,1)} %convolution_convert_fusion, f32[4096,1792]{1,0:T(8,128)} %fusion.103, bf16[1,4096,768]{1,2,0:T(8,128)(2,1)} %copy.20, f32[4096]{0:T(1024)S(1)} %copy-done.6), kind=kOutput, calls=%fused_computation.102 | convolution fusion | flops 11329142784 | bytes 53100544 | tf_op jit(solution)/shard_map/transpose(jvp())/dot_general | solution.py:22
  358.3 29.9 %fusion.89 = bf16[1,768,1792]{2,1,0:T(8,128)(2,1)} fusion(f32[4096,1792]{1,0:T(8,128)} %fusion.103, f32[4096,1792]{1,0:T(8,128)} %get-tuple-element.25, bf16[4096,1792]{1,0:T(8,128)(2,1)} %convolution_convert_fusion, bf16[1,4096,768]{1,2,0:T(8,128)(2,1)} %copy.20, f32[4096]{0:T(1024)S(1)} %copy-done.6), kind=kOutput, calls=%fused_computation.103 | convolution fusion | flops 11365842944 | bytes 82460672 | tf_op jit(solution)/shard_map/transpose(jvp())/dot_general | solution.py:21
  388.2 0.1 all-reduce.3.cloned.1.call-update
  388.2 285.7 %all-reduce.3.cloned.1.call-done = (bf16[1,768,1792]{2,1,0:T(8,128)(2,1)}, bf16[1,768,1792]{2,1,0:T(8,128)(2,1)}, bf16[1,768,1792]{2,1,0:T(8,128)(2,1)}, bf16[1,...) async-done(((bf16[1,768,1792]{2,1,0:T(8,128)(2,1)}, bf16[1,768,1792]{2,1,0:T(8,128)(2,1)}, bf16[1,768,1792]{2,1,0:T(8,128)(2,1)}, ...) | async-done | bytes 16515088 | tf_op jit(solution)/shard_map/psum | solution.py:50
  674.0 0.0 copy-start
  674.0 0.0 copy-start.1
  674.0 6.2 fusion.33
  680.1 6.0 fusion.32
  686.2 0.0 copy-done
  686.2 0.0 copy-done.1
  686.2 3.4 fusion.31
  691.6 22.2 %fusion.39 = (bf16[2,1792,768]{2,1,0:T(8,128)(2,1)}, f32[2,1792,768]{2,1,0:T(8,128)}, f32[2,1792,768]{2,1,0:T(8,128)}) fusion(bf16[2,1792,768]{2,1,0:T(8,128)(2,1)} %param.15, f32[]{:T(128)S(6)} %min_shard_map.3, bf16[1,1792,768]{2,1,0:T(8,128)(2,1)} %get-tuple-element.13, bf16[1,1792,768]{2,1,0:T(8,128)(2,1)} %get-tuple-element.14, ...), kind=kLoop, calls=%fused_computation.73 | loop fusion | flops 55050240 | bytes 60555268 | tf_op jit(solution)/shard_map/convert_element_type | solution.py:30
  713.8 36.7 %fusion.30 = (bf16[2,768,1792]{2,1,0:T(8,128)(2,1)}, f32[2,768,1792]{2,1,0:T(8,128)}, f32[2,768,1792]{2,1,0:T(8,128)}, bf16[2,768,1792]{2,1,0:T(8,128)(2,1)}, f3...) fusion(bf16[2,768,1792]{2,1,0:T(8,128)(2,1)} %param.13, f32[]{:T(128)S(6)} %min_shard_map.3, ...), kind=kLoop, calls=%fused_computation.64 | loop fusion | flops 110100480 | bytes 121110528 | tf_op jit(solution)/shard_map/convert_element_type | solution.py:30
  (6 shorter events, 0.0 us)
Async XLA Ops:
  7.2 666.8 %all-reduce.3.cloned.1.call-start = ((), (), s32[]{:S(2)}) async-start(), calls=%async_computation | async-start | bytes 33030144 | tf_op jit(solution)/shard_map/psum | solution.py:50
  20.0 43.6 %copy-start.5 = (f32[4096]{0:T(1024)}, f32[4096]{0:T(1024)S(1)}, u32[]{:S(2)}) copy-start(f32[4096]{0:T(1024)S(1)} %add_rsqrt_fusion) | copy-start | bytes 49156
  20.0 26.5 %slice-start.2 = ((s8[6291456]{0:T(1024)(128)(4,1)}), s8[2097152]{0:T(1024)(128)(4,1)S(1)}, s32[]{:S(2)}) async-start(s8[6291456]{0:T(1024)(128)(4,1)} %bitcast.84), calls=%async_computation.3 | async-start | bytes 4194304
  28.8 17.7 %slice-start.3 = ((s8[6291456]{0:T(1024)(128)(4,1)}), s8[4194304]{0:T(1024)(128)(4,1)S(1)}, s32[]{:S(2)}) async-start(s8[6291456]{0:T(1024)(128)(4,1)} %bitcast.84), calls=%async_computation.4 | async-start | bytes 8388608
  115.8 20.2 %copy-start.3 = (f32[4096]{0:T(1024)}, f32[4096]{0:T(1024)S(1)}, u32[]{:S(2)}) copy-start(f32[4096]{0:T(1024)S(1)} %get-tuple-element.26) | copy-start | bytes 49156
  249.9 39.4 %slice-start = ((s8[6291456]{0:T(1024)(128)(4,1)}), s8[4194304]{0:T(1024)(128)(4,1)S(1)}, s32[]{:S(2)}) async-start(s8[6291456]{0:T(1024)(128)(4,1)} %bitcast.82), calls=%async_computation.1 | async-start | bytes 8388608
  268.7 20.6 %copy-start.4 = (f32[4096]{0:T(1024)S(1)}, f32[4096]{0:T(1024)}, u32[]{:S(2)}) copy-start(f32[4096]{0:T(1024)} %copy-done.3) | copy-start | bytes 49156
  268.7 20.6 %slice-start.1 = ((s8[6291456]{0:T(1024)(128)(4,1)}), s8[2097152]{0:T(1024)(128)(4,1)S(1)}, s32[]{:S(2)}) async-start(s8[6291456]{0:T(1024)(128)(4,1)} %bitcast.82), calls=%async_computation.2 | async-start | bytes 4194304
  296.5 2.7 copy-start.2
  315.3 17.9 %copy-start.6 = (f32[4096]{0:T(1024)S(1)}, f32[4096]{0:T(1024)}, u32[]{:S(2)}) copy-start(f32[4096]{0:T(1024)} %copy-done.5) | copy-start | bytes 49156
  674.0 12.2 %copy-start = (bf16[1,768,1792]{2,1,0:T(8,128)(2,1)S(1)}, bf16[1,768,1792]{2,1,0:T(8,128)(2,1)}, u32[]{:S(2)}) copy-start(bf16[1,768,1792]{2,1,0:T(8,128)(2,1)} %get-tuple-element.9) | copy-start | bytes 8257540
  674.0 12.2 %copy-start.1 = (bf16[1,768,1792]{2,1,0:T(8,128)(2,1)S(1)}, bf16[1,768,1792]{2,1,0:T(8,128)(2,1)}, u32[]{:S(2)}) copy-start(bf16[1,768,1792]{2,1,0:T(8,128)(2,1)} %get-tuple-element.10) | copy-start | bytes 8257540
Sparse Core Ops, SparseCore 0:
  388.4 285.5 all-reduce.2
where the time goes:
time: 766 us; the launch traced here: 758 us
  matrix products  350 us (46%)
  waiting for transfers between devices  286 us (37%)
  other arithmetic  85.8 us (11%)
  local copies, waits for them, and re-layouts  20.1 us (3%)
  between operations  16.6 us (2%)
    psum x1, waiting for transfers between devices, step(): summed[number] = [lax.psum(by_w[name], 'dp') for name in NAMES]  286 us
    dot_general x5, matrix products, layer(): up = jnp.dot(a, w['w_up'], preferred_element_type=jnp.float32)  126 us
    dot_general x5, matrix products, layer(): gate = jnp.dot(a, w['w_gate'], preferred_element_type=jnp.float32)  126 us
    dot_general x5, matrix products, matmul(): jnp.dot(a, w, preferred_element_type=jnp.float32).astype(jnp.bfloat16)  97 us
    convert_element_type x2, other arithmetic, adamw(): return ((w - 0.02 * step).astype(jnp.bfloat16), m, v)  58.9 us
    unnamed x24, local copies, waits for them, and re-layouts  20.1 us
    reduce_sum x3, other arithmetic, step(): jnp.sum(g * g)  15.7 us
  transfers between devices with their start and end apart: 1, of which 1 were waited for; matrix products, arithmetic and copies ran while one was open for 0% of the time, Pallas kernels for 0%

commit v1 on v0

v1 whole, which is shorter than its diff:
```python
import functools

import jax
import jax.numpy as jnp
from jax import lax
from jax.experimental import pallas as pl
from jax.experimental.pallas import tpu as pltpu
from jax.sharding import PartitionSpec as P


F32, BF16 = jnp.float32, jnp.bfloat16
TILE = 512
SUB = 512
UNIT = 256
FULL_VMEM = 60 << 20
PIECES = {1: (2, 2, 3), 0: (3, 3, 1)}


def params(**kw):
    return pltpu.CompilerParams(vmem_limit_bytes=FULL_VMEM, **kw)


def cost(matmuls, moved, tokens, d, width):
    return pl.CostEstimate(flops=2 * matmuls * tokens * d * width, bytes_accessed=moved, transcendentals=0)


def dot(a, b, ca, cb):
    return lax.dot_general(a, b, (((ca,), (cb,)), ((), ())), preferred_element_type=F32)


def scale_of(wide):
    return lax.rsqrt(jnp.mean(wide * wide, -1, keepdims=True) + 1e-6)


def forward_kernel(x_ref, wg_ref, wu_ref, wd_ref, a_ref, h_ref, b_ref, gate_ref, up_ref, p_ref):
    rows = SUB
    for sub in range(x_ref.shape[0] // SUB):
        at = slice(sub * rows, (sub + 1) * rows)
        x = x_ref[at, :].astype(F32)
        a = (x * scale_of(x)).astype(BF16)
        a_ref[at, :] = a
        for j in range(p_ref.shape[1] // UNIT):
            cols = slice(j * UNIT, (j + 1) * UNIT)
            gate = dot(a, wg_ref[:, cols], 1, 0)
            up = dot(a, wu_ref[:, cols], 1, 0)
            gate_ref[at, cols] = gate
            up_ref[at, cols] = up
            p_ref[at, cols] = (gate * jax.nn.sigmoid(gate) * up).astype(BF16)
    for sub in range(x_ref.shape[0] // SUB):
        at = slice(sub * rows, (sub + 1) * rows)
        h = x_ref[at, :] + dot(p_ref[at, :], wd_ref[...], 1, 0).astype(BF16)
        h_ref[at, :] = h
        wide = h.astype(F32)
        b_ref[at, :] = (wide * scale_of(wide)).astype(BF16)


def forward(x, wg, wu, wd, layer):
    tokens, d = x.shape
    ff = wg.shape[2]
    rows = pl.BlockSpec((TILE, d), lambda t: (t, 0))
    hidden = pl.BlockSpec((TILE, ff), lambda t: (t, 0))
    whole = lambda r, c: pl.BlockSpec((None, r, c), lambda t: (layer, 0, 0), pipeline_mode=pl.Buffered(1))
    out = jax.ShapeDtypeStruct((tokens, d), BF16)
    wide = jax.ShapeDtypeStruct((tokens, ff), F32)
    return pl.pallas_call(
        forward_kernel,
        grid=(tokens // TILE,),
        in_specs=[rows, whole(d, ff), whole(d, ff), whole(ff, d)],
        out_specs=[rows] * 3 + [hidden] * 2,
        out_shape=[out] * 3 + [wide] * 2,
        scratch_shapes=[pltpu.VMEM((TILE, ff), BF16)],
        compiler_params=params(dimension_semantics=("arbitrary",)),
        cost_estimate=cost(3, 8 * tokens * d + 6 * d * ff, tokens, d, ff),
        name="forward",
    )(x, wg, wu, wd)


def remote(src, dst, sems, i, to):
    send, recv = sems
    return pltpu.make_async_remote_copy(
        src_ref=src, dst_ref=dst, send_sem=send.at[i], recv_sem=recv.at[i], device_id={"dp": to}, device_id_type=pl.DeviceIdType.MESH
    )


def around(n):
    me = lax.axis_index("dp")
    return lax.rem(me + 1, n), lax.rem(me + n - 1, n)


class Sum:
    def __init__(self, parts, n, middle):
        self.operands, self.n, self.middle = list(parts), n, middle
        half = parts[0].shape[1:]
        self.half = half
        self.outs = [jax.ShapeDtypeStruct((2, *half), BF16), jax.ShapeDtypeStruct((8, half[-1]), F32)]
        self.out_specs = [pl.BlockSpec((2, *half), lambda t: (0,) * 4), pl.BlockSpec((8, half[-1]), lambda t: (0, 0))]
        self.scratch = [pltpu.VMEM((k, *half), BF16) for k in (2, 2, 4, 2, 2)]
        self.scratch += [pltpu.SemaphoreType.DMA((6,)), pltpu.SemaphoreType.DMA((6,)), pltpu.SemaphoreType.DMA((1,))]

    def bind(self, refs):
        to_right, to_left, rest, self.share, self.squares, self.from_left, self.from_right, self.rest, self.sums, self.second, *sems, local = refs
        right, left = around(self.n)
        self.copies = [
            remote(to_right.at[0], self.from_left.at[0], sems, 0, right),
            remote(to_left.at[0], self.from_right.at[0], sems, 1, left),
            remote(to_right.at[1], self.from_left.at[1], sems, 2, right),
            remote(to_left.at[1], self.from_right.at[1], sems, 3, left),
            remote(self.sums.at[0], self.second.at[0], sems, 4, right),
            remote(self.sums.at[1], self.second.at[1], sems, 5, left),
        ]
        self.local = pltpu.make_async_copy(rest, self.rest, local.at[0])

    def start(self):
        self.local.start()
        for copy in self.copies[:4]:
            copy.start()

    def step(self):
        self.local.wait()
        for i, came in enumerate((self.from_left, self.from_right)):
            self.copies[i].wait_recv()

            @pl.loop(0, self.half[0])
            def _(k):
                self.sums[i, k] = (self.rest[i, k].astype(F32) + came[0, k].astype(F32)).astype(BF16)

            self.copies[4 + i].start()

    def end(self):
        for copy in self.copies[2:]:
            copy.wait_recv()
        self.squares[...] = jnp.zeros_like(self.squares)
        for i, came in enumerate((self.from_right, self.from_left)):

            @pl.loop(0, self.half[0])
            def _(k):
                whole = self.rest[2 + i, k].astype(F32) + came[1, k].astype(F32) + self.second[i, k].astype(F32)
                self.share[i, k] = whole.astype(BF16)
                rounded = whole.astype(BF16).astype(F32)
                self.squares[...] += jnp.sum((rounded * rounded).reshape(-1, 8, rounded.shape[-1]), 0)

        for copy in self.copies:
            copy.wait_send()


class Gather:
    def __init__(self, share, n, middle):
        self.operands, self.n, self.middle = [share], n, middle
        self.outs = [jax.ShapeDtypeStruct(share.shape, BF16)] * 3
        self.out_specs = [pl.BlockSpec(memory_space=pl.ANY)] * 3
        self.scratch = [pltpu.SemaphoreType.DMA((6,)), pltpu.SemaphoreType.DMA((6,))]

    def bind(self, refs):
        share, after, far, before, *sems = refs
        right, left = around(self.n)
        self.copies = [
            remote(share.at[0], before.at[0], sems, 0, right),
            remote(share.at[1], after.at[1], sems, 1, left),
            remote(share.at[1], before.at[1], sems, 2, right),
            remote(share.at[0], after.at[0], sems, 3, left),
            remote(before.at[0], far.at[0], sems, 4, right),
            remote(after.at[1], far.at[1], sems, 5, left),
        ]

    def start(self):
        for copy in self.copies[:4]:
            copy.start()

    def step(self):
        for i in range(2):
            self.copies[i].wait_recv()
            self.copies[4 + i].start()

    def end(self):
        for copy in self.copies[2:]:
            copy.wait_recv()
        for copy in self.copies:
            copy.wait_send()


def run(body, n, steps, ins, in_specs, outs, out_specs, scratch, tasks, number, **kw):
    groups = [(ins, outs, scratch), *((t.operands, t.outs, t.scratch) for t in tasks)]

    def kernel(*refs):
        at, dealt = 0, [[] for _ in groups]
        for which in range(3):
            for i, group in enumerate(groups):
                dealt[i] += refs[at : at + len(group[which])]
                at += len(group[which])
        t = pl.program_id(0)
        for task, own in zip(tasks, dealt[1:], strict=True):
            task.bind(own)
        if tasks:

            @pl.when(t == 0)
            def _():
                barrier = pltpu.get_barrier_semaphore()
                for to in around(n):
                    pl.semaphore_signal(barrier, inc=1, device_id={"dp": to}, device_id_type=pl.DeviceIdType.MESH)
                pl.semaphore_wait(barrier, 2)
                for task in tasks:
                    task.start()

            for task in tasks:
                pl.when(t == task.middle)(task.step)
        body(*dealt[0])
        for task in tasks:
            pl.when(t == steps - 1)(task.end)

    anywhere = pl.BlockSpec(memory_space=pl.ANY)
    out = pl.pallas_call(
        kernel,
        grid=(steps,),
        in_specs=list(in_specs) + [anywhere for t in tasks for _ in t.operands],
        out_specs=list(out_specs) + [s for t in tasks for s in t.out_specs],
        out_shape=list(outs) + [o for t in tasks for o in t.outs],
        scratch_shapes=list(scratch) + [s for t in tasks for s in t.scratch],
        compiler_params=params(
            dimension_semantics=("arbitrary",), **(dict(collective_id=number, has_side_effects=True) if tasks else {})
        ),
        **kw,
    )(*ins, *(o for t in tasks for o in t.operands))
    out, given = list(out), []
    own, out = out[: len(outs)], out[len(outs) :]
    for t in tasks:
        given.append(out[: len(t.outs)])
        out = out[len(t.outs) :]
    return own, *given


def piece_kernel(units, start, n, saved, a_ref, dy_ref, *refs):
    if saved:
        gate_ref, up_ref, wd_ref, to_right, to_left, rest, acc, acc_d, p_s, dgu_ref = refs
    else:
        wg_ref, wu_ref, wd_ref, to_right, to_left, rest, dgu_ref, acc, acc_d, p_s = refs
    width = units * UNIT
    t = pl.program_id(0)

    @pl.when(t == 0)
    def _():
        acc[...] = jnp.zeros_like(acc)
        acc_d[...] = jnp.zeros_like(acc_d)

    def accumulate(j, sub):
        at = slice(sub * SUB, (sub + 1) * SUB)
        cols = slice(j * UNIT, (j + 1) * UNIT)
        ups = slice(width + j * UNIT, width + (j + 1) * UNIT)
        acc[:, cols] += dot(a_ref[at, :], dgu_ref[at, cols], 0, 0)
        acc[:, ups] += dot(a_ref[at, :], dgu_ref[at, ups], 0, 0)
        acc_d[cols, :] += dot(p_s[at, cols], dy_ref[at, :], 0, 0)

    before = None
    for sub in range(a_ref.shape[0] // SUB):
        for j in range(units):
            at = slice(sub * SUB, (sub + 1) * SUB)
            cols = slice(j * UNIT, (j + 1) * UNIT)
            there = slice((start + j) * UNIT, (start + j + 1) * UNIT)
            gate = gate_ref[at, there] if saved else dot(a_ref[at, :], wg_ref[:, there], 1, 0)
            up = up_ref[at, there] if saved else dot(a_ref[at, :], wu_ref[:, there], 1, 0)
            dp = dot(dy_ref[at, :], wd_ref[there, :], 1, 1).astype(BF16).astype(F32)
            s = jax.nn.sigmoid(gate)
            act = gate * s
            p_s[at, cols] = (act * up).astype(BF16)
            dgu_ref[at, width + j * UNIT : width + (j + 1) * UNIT] = (dp * act).astype(BF16)
            dgu_ref[at, cols] = (dp * up * (s * (1.0 + gate * (1.0 - s)))).astype(BF16)
            if before:
                accumulate(*before)
            before = j, sub
    accumulate(*before)

    @pl.when(t == pl.num_programs(0) - 1)
    def _():
        part = to_right.shape[2]
        small = UNIT // (2 * n)
        me = lax.axis_index("dp")

        def put(ref, by, half):
            at = (lax.rem(me + by, n) * 2 + half)
            rows = pl.ds(pl.multiple_of(at * part, part), part)
            for u in range(units):
                for which in range(2):
                    low = which * width + u * UNIT
                    ref[3 * u + which] = acc[rows, low : low + UNIT].astype(BF16)
                thin = pl.ds(pl.multiple_of(u * UNIT + at * small, small), small)
                for b in range(part // small):
                    ref[3 * u + 2, b * small : (b + 1) * small, :] = acc_d[thin, b * UNIT : (b + 1) * UNIT].astype(BF16)

        put(to_right.at[0], 2, 0)
        put(to_right.at[1], 1, 1)
        put(to_left.at[0], 2, 1)
        put(to_left.at[1], n - 1, 0)
        put(rest.at[0], 1, 0)
        put(rest.at[1], n - 1, 1)
        put(rest.at[2], 0, 0)
        put(rest.at[3], 0, 1)


def piece(a, dy, weights, saved, layer, start, units, n, tasks=(), number=0):
    tokens, d = a.shape
    width = units * UNIT
    tile = TILE
    rows = pl.BlockSpec((tile, d), lambda t: (t, 0))
    part = d // (2 * n)
    cols = pl.BlockSpec((None, d, weights[0].shape[2]), lambda t: (layer, 0, 0), pipeline_mode=pl.Buffered(1))
    down = pl.BlockSpec((None, weights[0].shape[2], d), lambda t: (layer, 0, 0), pipeline_mode=pl.Buffered(1))
    kept = pl.BlockSpec((tile, weights[0].shape[2]), lambda t: (t, 0))
    both = pl.BlockSpec((tile, 2 * width), lambda t: (t, 0))
    shapes = [(2, 3 * units, part, UNIT)] * 2 + [(4, 3 * units, part, UNIT)]
    outs = [jax.ShapeDtypeStruct(s, BF16) for s in shapes]
    specs = [pl.BlockSpec(s, lambda t: (0,) * 4) for s in shapes]
    scratch = [pltpu.VMEM((d, 2 * width), F32), pltpu.VMEM((width, d), F32), pltpu.VMEM((tile, width), BF16)]
    if saved:
        ins, operands = [kept, kept], saved
        scratch.append(pltpu.VMEM((tile, 2 * width), BF16))
    else:
        ins, operands = [cols, cols], weights[:2]
        outs.append(jax.ShapeDtypeStruct((tokens, 2 * width), BF16))
        specs.append(both)
    return run(
        functools.partial(piece_kernel, units, start, n, bool(saved)),
        n,
        tokens // tile,
        (a, dy, *operands, weights[2]),
        [rows, rows] + ins + [down],
        outs,
        specs,
        scratch,
        tasks,
        number,
        cost_estimate=cost(4 if saved else 6, 4 * tokens * d + 12 * d * width, tokens, d, width),
        name=f"piece_{layer}_{start}",
    )


def back_kernel(count, *refs):
    parts = refs[:count]
    wg_ref, wu_ref, h_ref, dy_ref, out_ref = refs[count:]

    rows = SUB
    for sub in range(h_ref.shape[0] // SUB):
        span = slice(sub * rows, (sub + 1) * rows)

        def back(which, w_ref):
            total, at = None, 0
            for part in parts:
                width = part.shape[1] // 2
                term = dot(part[span, which * width : (which + 1) * width], w_ref[:, at : at + width], 1, 1)
                total, at = term if total is None else total + term, at + width
            return total.astype(BF16)

        da = (back(0, wg_ref) + back(1, wu_ref)).astype(F32)
        h = h_ref[span, :].astype(F32)
        scale = scale_of(h)
        along = jnp.mean(da * h, -1, keepdims=True)
        out_ref[span, :] = dy_ref[span, :] + (da * scale - h * (scale * scale * scale * along)).astype(BF16)


def back(parts, wg, wu, h, dy, layer, n, tasks=(), number=0):
    tokens, d = h.shape
    ff = wg.shape[2]
    rows = pl.BlockSpec((TILE, d), lambda t: (t, 0))
    whole = pl.BlockSpec((None, d, ff), lambda t: (layer, 0, 0), pipeline_mode=pl.Buffered(1))
    hidden = [pl.BlockSpec((TILE, g.shape[1]), lambda t: (t, 0)) for g in parts]
    return run(
        functools.partial(back_kernel, len(parts)),
        n,
        tokens // TILE,
        (*parts, wg, wu, h, dy),
        hidden + [whole, whole, rows, rows],
        [jax.ShapeDtypeStruct((tokens, d), BF16)],
        [rows],
        (),
        tasks,
        number,
        cost_estimate=cost(2, 6 * tokens * d + 4 * d * ff + 4 * tokens * ff, tokens, d, ff),
        name="back",
    )


class Finish(Sum):
    def __init__(self, parts, n, others, count):
        super().__init__(parts, n, 0)
        self.operands, self.count, self.others = self.operands + list(others), count, len(others)
        tile = (8, others[0].shape[1])
        self.outs.append(jax.ShapeDtypeStruct(tile, F32))
        self.out_specs.append(pl.BlockSpec(tile, lambda t: (0, 0)))
        self.scratch += [pltpu.VMEM((n, *tile), F32), pltpu.VMEM((len(others), *tile), F32), pltpu.SemaphoreType.DMA((1,))]
        self.scratch += [pltpu.SemaphoreType.DMA((n,)), pltpu.SemaphoreType.DMA((n,))]


def finish_kernel(task, refs):
    k = task.others
    parts, others, share, squares, factor = refs[:3], refs[3 : 3 + k], refs[3 + k], refs[4 + k], refs[5 + k]
    rest = refs[6 + k :]
    terms, held, local, send, recv = rest[8:]
    n = task.n
    me = lax.axis_index("dp")
    barrier = pltpu.get_barrier_semaphore()
    for by in range(1, n):
        pl.semaphore_signal(barrier, inc=1, device_id={"dp": lax.rem(me + by, n)}, device_id_type=pl.DeviceIdType.MESH)
    pl.semaphore_wait(barrier, n - 1)
    task.bind([*parts, share, squares, *rest[:8]])
    task.start()
    for i, other in enumerate(others):
        copy = pltpu.make_async_copy(other, held.at[i], local.at[0])
        copy.start()
        copy.wait()
    task.step()
    task.end()
    total = squares[...]
    for i in range(k):
        total += held[i]
    terms[me] = total
    copies = [remote(terms.at[me], terms.at[me], (send, recv), by, lax.rem(me + by, n)) for by in range(1, n)]
    for copy in copies:
        copy.start()
    for by in range(1, n):
        sender = lax.rem(me + n - by, n)
        remote(terms.at[sender], terms.at[sender], (send, recv), by, lax.rem(me + by, n)).wait_recv()
    everything = terms[0]
    for i in range(1, n):
        everything += terms[i]
    everything = jnp.sum(jnp.sum(everything, 0, keepdims=True), 1, keepdims=True)
    factor[...] = jnp.broadcast_to(jnp.minimum(1.0, 0.5 * lax.rsqrt(everything / task.count + 1e-30)), factor.shape)
    for copy in copies:
        copy.wait_send()


def finish(parts, n, others, count, number):
    task = Finish(parts, n, others, count)
    anywhere = pl.BlockSpec(memory_space=pl.ANY)
    return pl.pallas_call(
        lambda *refs: finish_kernel(task, refs),
        grid=(1,),
        in_specs=[anywhere] * len(task.operands),
        out_specs=task.out_specs,
        out_shape=task.outs,
        scratch_shapes=task.scratch,
        compiler_params=params(collective_id=number, has_side_effects=True),
        cost_estimate=pl.CostEstimate(flops=4 * 10**9, bytes_accessed=10**6, transcendentals=0),
        name="finish",
    )(*task.operands)


def adamw_kernel(n, count, me_ref, factor_ref, *refs):
    grads, ins, outs = refs[:count], refs[count : count + 9], refs[-9:]
    factor = factor_ref[0:1, 0:1]
    me = me_ref[0]
    for number in range(2 * n):
        at = lax.rem(me + number // 2, n) * 2 + number % 2
        ref = grads[number // 2].at[number % 2] if count == n else grads[number]
        for which in range(3):
            w_ref, m_ref, v_ref = (ins[which + 3 * i] for i in range(3))
            w_out, m_out, v_out = (outs[which + 3 * i] for i in range(3))
            part = ref.shape[1]
            if which < 2:
                spots = [((pl.ds(pl.multiple_of(at * part, part), part), slice(None)), ref[which])]
            else:
                small = w_ref.shape[0] // (2 * n)
                spots = [
                    ((pl.ds(pl.multiple_of(at * small, small), small), slice(b * UNIT, (b + 1) * UNIT)), ref[which, b * small : (b + 1) * small])
                    for b in range(part // small)
                ]
            for spot, g in spots:
                g = g.astype(F32) * factor
                m = 0.9 * m_ref[spot] + 0.1 * g
                v = 0.95 * v_ref[spot] + 0.05 * g * g
                w = w_ref[spot].astype(F32)
                m_out[spot] = m
                v_out[spot] = v
                w_out[spot] = (w - 0.02 * (m * lax.rsqrt(v + 1e-8) + 0.1 * w)).astype(BF16)


def adamw(arrays, done, grads, me, factor, layer, start, n):
    d = arrays[0].shape[1]
    units = grads[0].shape[-3] // 3
    wide = pl.BlockSpec((None, d, UNIT), lambda s, me: (layer, 0, start + s))
    tall = pl.BlockSpec((None, UNIT, d), lambda s, me: (layer, start + s, 0))
    specs = [wide, wide, tall] * 3
    if len(grads) == n:
        grad = pl.BlockSpec((2, 3) + grads[0].shape[2:], lambda s, me: (0, s, 0, 0))
    else:
        grad = pl.BlockSpec((3,) + grads[0].shape[1:], lambda s, me: (s, 0, 0))
    held = [] if done is None else list(done)
    count = len(grads)
    return pl.pallas_call(
        functools.partial(adamw_kernel, n, count),
        grid_spec=pltpu.PrefetchScalarGridSpec(
            num_scalar_prefetch=1,
            grid=(units,),
            in_specs=[pl.BlockSpec(factor.shape, lambda s, me: (0, 0))]
            + [grad] * count
            + specs
            + [pl.BlockSpec(memory_space=pl.ANY)] * len(held),
            out_specs=specs,
        ),
        out_shape=[jax.ShapeDtypeStruct(a.shape, a.dtype) for a in arrays],
        input_output_aliases={2 + count + 9 + i: i for i in range(len(held))},
        compiler_params=params(dimension_semantics=("arbitrary",)),
        cost_estimate=pl.CostEstimate(flops=10**9 * 4 * units, bytes_accessed=22 * 3 * units * UNIT * d, transcendentals=0),
    )(me[None], factor, *grads, *arrays, *held)


def tie(value, *others):
    return lax.optimization_barrier((value, *others))[0]


def solution(mesh):
    n = mesh.shape["dp"]

    def step(x, dy, *arrays):
        weights = arrays[:3]
        wg, wu, wd = weights
        x, dy = x[0], dy[0]
        me = lax.axis_index("dp")
        count = sum(a.size for a in weights)

        def send(array, by):
            return lax.ppermute(array, "dp", [(i, (i + by) % n) for i in range(n)])

        def spread(a, b):
            ra, lb = send(a, 1), send(b, -1)
            rb, la = send(b, 1), send(a, -1)
            return a, b, la, lb, ra, rb

        def onward(got):
            a, b, la, lb, ra, rb = got
            return a, b, la, lb, send(ra, 1), send(lb, -1), ra, rb

        starts = {(layer, i): sum(PIECES[layer][:i]) for layer in PIECES for i in range(len(PIECES[layer]))}
        A, B, C, D, E, F = starts

        def make(key, a, by_h, kept=(), tasks=(), number=0):
            units = PIECES[key[0]][key[1]]
            return piece(a, by_h, weights, kept, key[0], starts[key], units, n, tasks, number)

        a0, h1, a1, gate, up = forward(x, wg, wu, wd, 0)
        (*pa, da), = make(A, a1, dy)
        (*pb, db), (sa, qa) = make(B, a1, dy, (), [Sum(pa, n, 3)], 1)
        (*pc, dc), (sb, qb), ga = make(C, a1, dy, (), [Sum(pb, n, 2), Gather(sa, n, 4)], 2)
        (by_h,), (sc, qc) = back((da, db, dc), wg, wu, h1, dy, 1, n, [Sum(pc, n, 3)], 3)
        pd, gb, gc = make(D, a0, by_h, (gate, up), [Gather(sb, n, 3), Gather(sc, n, 7)], 4)
        pe, (sd, qd) = make(E, a0, by_h, (gate, up), [Sum(pd, n, 3)], 5)
        pf, (se, qe) = make(F, a0, by_h, (gate, up), [Sum(pe, n, 3)], 6)
        sf, _, factor = finish(pf, n, (qa, qb, qc, qd, qe), count, 7)

        got = {D: spread(tie(sd[0], factor), sd[1]), E: spread(tie(se[0], factor), se[1]), F: spread(sf[0], sf[1])}
        step_on = lambda key, done, grads: adamw(arrays, done, grads, me, factor, key[0], starts[key], n)
        done = step_on(A, None, (sa, *ga))
        done = step_on(B, done, (sb, *gb))
        done = step_on(C, done, (sc, *gc))
        for key in (D, E, F):
            done = step_on(key, done, onward(got[key]))
        return tuple(done)

    return jax.shard_map(
        step,
        mesh=mesh,
        in_specs=(P(("rep", "dp"), None, None),) * 2 + (P(None, None, None),) * 9,
        out_specs=(P("rep", None, None),) * 9,
        check_vma=False,
    )
```

time: 766 us -> 450 us (0.59)
  Pallas kernels: 0 us -> 412 us
  matrix products: 350 us -> 0 us
  waiting for transfers between devices: 286 us -> 0.05 us
  other arithmetic: 85.8 us -> 0 us
  starting transfers between devices: 0.06 us -> 24.9 us
  local copies, waits for them, and re-layouts: 20.1 us -> 3.86 us
  between operations: 16.6 us -> 1.26 us
    pallas_call x0 -> x15, Pallas kernels: none -> 412 us  [the longest x7 279 us: run(): pl.pallas_call(kernel, grid=(steps,), in_specs=list(in_specs) + [anywhere...]
    dot_general x15 -> x0, matrix products: 350 us -> none  [the longest x5 126 us: layer(): up = jnp.dot(a, w['w_up'], preferred_element_type=jnp.float32)]
    psum x1 -> x0, waiting for transfers between devices: 286 us -> none  [step(): summed[number] = [lax.psum(by_w[name], 'dp') for name in NAMES]]
    convert_element_type x2 -> x0, other arithmetic: 58.9 us -> none  [adamw(): return ((w - 0.02 * step).astype(jnp.bfloat16), m, v)]
    ppermute x0 -> x18, starting transfers between devices: none -> 24.9 us  [send(): return lax.ppermute(array, 'dp', [(i, (i + by) % n) for i in range(n)])]
    reduce_sum x4 -> x0, other arithmetic: 19.7 us -> none  [the longest x3 15.7 us: step(): jnp.sum(g * g)]
    unnamed x24 -> x42, local copies, waits for them, and re-layouts: 20.1 us -> 1.6 us
  transfers between devices with their start and end apart: 1 -> 18, of which waited for: 1 -> 0; matrix products, arithmetic and copies ran while one was open for 0% -> 0% of each run, Pallas kernels for 0% -> 15%
where the time goes in v1:
time: 450 us; the launch traced here: 442 us
  Pallas kernels  412 us (92%)
  starting transfers between devices  24.9 us (6%)
    pallas_call x7, Pallas kernels, run(): pl.pallas_call(kernel, grid=(steps,), in_specs=list(in_specs) + [anywhere...  279 us
    pallas_call x6, Pallas kernels, adamw(): pl.pallas_call(functools.partial(adamw_kernel, n, count), grid_spec=pltpu...  70.7 us
    pallas_call x1, Pallas kernels, forward(): pl.pallas_call(forward_kernel, grid=(tokens // TILE,), in_specs=[rows, wh...  45.9 us
    ppermute x18, starting transfers between devices, send(): return lax.ppermute(array, 'dp', [(i, (i + by) % n) for i in range(n)])  24.9 us
    pallas_call x1, Pallas kernels, finish(): pl.pallas_call(lambda *refs: finish_kernel(task, refs), grid=(1,), in_spe...  16.8 us
  transfers between devices with their start and end apart: 18, of which 0 were waited for; matrix products, arithmetic and copies ran while one was open for 0% of the time, Pallas kernels for 15%

profile of v1, /device:TPU:112, one launch (start us, length us, event | category | flops | bytes accessed | tf_op | source)
XLA Modules:
  0.0 442.2 jit_solution(2671885625574010943)
XLA Ops:
  0.6 45.9 %forward.1 = (bf16[4096,768]{1,0:T(8,128)(2,1)}, bf16[4096,768]{1,0:T(8,128)(2,1)}, bf16[4096,768]{1,0:T(8,128)(2,1)}, f32[4096,1792]{1,0:T(8,128)}, f32[4096,1792]{1,0:T(8,128)}) custom-call(bf16[4096,768]{1,0:T(8,128)(2,1)} %bitcast.15, bf16[2,768,1792]{2,1,0:T(8,128)(2,1)} %refs_8_.11, bf16[2,768,1792]{2,1,0:T(8,128)(2,1)} %refs_9_.11, ...), custom_call_target="tpu_custom_call" | custom-call | flops 33822867456 | bytes 33423360 | tf_op jit(solution)/shard_map/forward/pallas_call | solution.py:65
  46.5 28.7 %piece_1_0.1 = (bf16[2,6,96,256]{3,2,1,0:T(8,128)(2,1)}, bf16[2,6,96,256]{3,2,1,0:T(8,128)(2,1)}, bf16[4,6,96,256]{3,2,1,0:T(8,128)(2,1)}, bf16[4096,1024]{1,0:T(8,128)(2,1)}) custom-call(bf16[4096,768]{1,0:T(8,128)(2,1)} %get-tuple-element.105.refs_0_, bf16[4096,768]{1,0:T(8,128)(2,1)} %bitcast.16, bf16[2,768,1792]{2,1,0:T(8,128)(2,1)} %refs_8_.11, ...), custom_call_target="tpu_custom_call" | custom-call | flops 19327352832 | bytes 17301504 | tf_op jit(solution)/shard_map/piece_1_0/pallas_call | solution.py:211
  75.2 33.9 %piece_1_2.1 = (bf16[2,6,96,256]{3,2,1,0:T(8,128)(2,1)}, bf16[2,6,96,256]{3,2,1,0:T(8,128)(2,1)}, bf16[4,6,96,256]{3,2,1,0:T(8,128)(2,1)}, bf16[4096,1024]{1,0:T...) custom-call(bf16[4096,768]{1,0:T(8,128)(2,1)} %get-tuple-element.105.refs_0_, ...), custom_call_target="tpu_custom_call" | custom-call | flops 19327352832 | bytes 17301504 | tf_op jit(solution)/shard_map/piece_1_2/pallas_call | solution.py:211
  109.1 48.9 %piece_1_4.1 = (bf16[2,9,96,256]{3,2,1,0:T(8,128)(2,1)}, bf16[2,9,96,256]{3,2,1,0:T(8,128)(2,1)}, bf16[4,9,96,256]{3,2,1,0:T(8,128)(2,1)}, bf16[4096,1536]{1,0:T...) custom-call(bf16[4096,768]{1,0:T(8,128)(2,1)} %get-tuple-element.105, ...), custom_call_target="tpu_custom_call" | custom-call | flops 28991029248 | bytes 19660800 | tf_op jit(solution)/shard_map/piece_1_4/pallas_call | solution.py:211
  158.0 38.4 %back.1 = (bf16[4096,768]{1,0:T(8,128)(2,1)}, bf16[2,9,96,256]{3,2,1,0:T(8,128)(2,1)}, f32[8,256]{1,0:T(8,128)}) custom-call(bf16[4096,1024]{1,0:T(8,128)(2,1)} %get-tuple-element.106.refs_0_, bf16[4096,1024]{1,0:T(8,128)(2,1)} %get-tuple-element.110.refs_1_, bf16[4096,1536]{1,0:T(8,128)(2,1)} %get-tuple-element.115.refs_2_, bf16[2,768,1792]{2,1,0:T(8,128)(2,1)} %refs_8_.11, ...), custom_call_target="tpu_custom_call" | custom-call | flops 22548578304 | bytes 53739520 | tf_op jit(solution)/shard_map/back/pallas_call | solution.py:211
  196.4 56.1 %piece_0_0.1 = (bf16[2,9,96,256]{3,2,1,0:T(8,128)(2,1)}, bf16[2,9,96,256]{3,2,1,0:T(8,128)(2,1)}, bf16[4,9,96,256]{3,2,1,0:T(8,128)(2,1)}, bf16[2,6,96,256]{3,2,...) custom-call(bf16[4096,768]{1,0:T(8,128)(2,1)} %get-tuple-element.104, ...), custom_call_target="tpu_custom_call" | custom-call | flops 19327352832 | bytes 19660800 | tf_op jit(solution)/shard_map/piece_0_0/pallas_call | solution.py:211
  252.4 38.8 %piece_0_3.1 = (bf16[2,9,96,256]{3,2,1,0:T(8,128)(2,1)}, bf16[2,9,96,256]{3,2,1,0:T(8,128)(2,1)}, bf16[4,9,96,256]{3,2,1,0:T(8,128)(2,1)}, bf16[2,9,96,256]{3,2,1,0:T(8,128)(2,1)}, f32[8,256]{1,0:T(8,128)}) custom-call(bf16[4096,768]{1,0:T(8,128)(2,1)} %get-tuple-element.104.refs_0_, bf16[4096,768]{1,0:T(8,128)(2,1)} %get-tuple-element.120.refs_1_, ...), custom_call_target="tpu_custom_call" | custom-call | flops 19327352832 | bytes 19660800 | tf_op jit(solution)/shard_map/piece_0_3/pallas_call | solution.py:211
  291.2 1.2 slice_bitcast_fusion
  292.5 34.1 %piece_0_6.1 = (bf16[2,3,96,256]{3,2,1,0:T(8,128)(2,1)}, bf16[2,3,96,256]{3,2,1,0:T(8,128)(2,1)}, bf16[4,3,96,256]{3,2,1,0:T(8,128)(2,1)}, bf16[2,9,96,256]{3,2,1,0:T(8,128)(2,1)}, f32[8,256]{1,0:T(8,128)}) custom-call(bf16[4096,768]{1,0:T(8,128)(2,1)} %get-tuple-element.104.refs_0_, bf16[4096,768]{1,0:T(8,128)(2,1)} %get-tuple-element.120.refs_1_, ...), custom_call_target="tpu_custom_call" | custom-call | flops 6442450944 | bytes 14942208 | tf_op jit(solution)/shard_map/piece_0_6/pallas_call | solution.py:211
  326.6 16.8 %finish.1 = (bf16[2,3,96,256]{3,2,1,0:T(8,128)(2,1)}, f32[8,256]{1,0:T(8,128)}, f32[8,256]{1,0:T(8,128)}) custom-call(bf16[2,3,96,256]{3,2,1,0:T(8,128)(2,1)} %get-tuple-element.131.refs_0_, bf16[2,3,96,256]{3,2,1,0:T(8,128)(2,1)} %get-tuple-element.132.refs_1_, bf16[4,3,96,256]{3,2,1,0:T(8,128)(2,1)} %get-tuple-element.133.refs_2_, ...), custom_call_target="tpu_custom_call" | custom-call | flops 4000000000 | bytes 1000000 | tf_op jit(solution)/shard_map/finish/pallas_call | solution.py:432
  343.4 0.5 collective-permute-start.14
  343.8 2.9 collective-permute-start.12
  346.7 1.3 collective-permute-start.13
  348.0 0.7 collective-permute-start.17
  348.7 1.0 slice_bitcast_fusion.4
  349.8 0.1 collective-permute-start.2
  349.9 9.8 %shard_map.178 = (bf16[2,768,1792]{2,1,0:T(8,128)(2,1)}, bf16[2,768,1792]{2,1,0:T(8,128)(2,1)}, bf16[2,1792,768]{2,1,0:T(8,128)(2,1)}, f32[2,768,1792]{2,1,0:T(8...) custom-call(s32[1]{0:T(128)} %bitcast.me_ref, ...), custom_call_target="tpu_custom_call" | custom-call | flops 8000000000 | bytes 25952256 | tf_op jit(solution)/shard_map/pallas_call | solution.py:486
  359.7 9.9 %shard_map.179 = (bf16[2,768,1792]{2,1,0:T(8,128)(2,1)}, bf16[2,768,1792]{2,1,0:T(8,128)(2,1)}, bf16[2,1792,768]{2,1,0:T(8,128)(2,1)}, f32[2,768,1792]{2,1,0:T(8...) custom-call(s32[1]{0:T(128)} %bitcast.me_ref, ...), custom_call_target="tpu_custom_call", output_to_operand_aliasing={{0}: (15, {}), {1}: (16, {}), {2}: (17, {}), {3}: (18, {}),... | custom-call | flops 8000000000 | bytes 25952256 | tf_op jit(solution)/shard_map/pallas_call | solution.py:486
  369.6 0.1 slice_bitcast_fusion.2
  369.7 0.0 collective-permute-done.2.refs_6_
  369.7 0.7 collective-permute-start.8
  370.4 0.0 collective-permute-done.14.refs_6_
  370.4 2.6 collective-permute-start.7
  373.1 0.7 collective-permute-start.15
  373.8 0.0 collective-permute-done.13.refs_3_
  373.8 2.6 collective-permute-start.16
  376.3 14.9 %shard_map.180 = (bf16[2,768,1792]{2,1,0:T(8,128)(2,1)}, bf16[2,768,1792]{2,1,0:T(8,128)(2,1)}, bf16[2,1792,768]{2,1,0:T(8,128)(2,1)}, f32[2,768,1792]{2,1,0:T(8...) custom-call(s32[1]{0:T(128)} %bitcast.me_ref, ...), custom_call_target="tpu_custom_call", output_to_operand_aliasing={{0}: (15, {}), {1}: (16, {}), {2}: (17, {}), {3}: (18, {}),... | custom-call | flops 12000000000 | bytes 38928384 | tf_op jit(solution)/shard_map/pallas_call | solution.py:486
  391.3 0.8 collective-permute-start.6
  392.1 1.4 collective-permute-start.11
  393.5 0.0 collective-permute-done.7.refs_3_
  393.5 1.9 collective-permute-start.1
  395.4 0.0 collective-permute-done.15.refs_4_
  395.4 0.1 collective-permute-start.9
  395.5 0.0 collective-permute-done.16.refs_5_
  395.5 3.1 collective-permute-start.10
  398.6 14.8 %shard_map.181 = (bf16[2,768,1792]{2,1,0:T(8,128)(2,1)}, bf16[2,768,1792]{2,1,0:T(8,128)(2,1)}, bf16[2,1792,768]{2,1,0:T(8,128)(2,1)}, f32[2,768,1792]{2,1,0:T(8...) custom-call(s32[1]{0:T(128)} %bitcast.me_ref, ...), custom_call_target="tpu_custom_call", output_to_operand_aliasing={{0}: (19, {}), {1}: (20, {}), {2}: (21, {}), {3}: (22, {}),... | custom-call | flops 12000000000 | bytes 38928384 | tf_op jit(solution)/shard_map/pallas_call | solution.py:486
  413.5 0.1 collective-permute-start
  413.7 2.0 collective-permute-start.5
  415.7 0.0 collective-permute-done.11.refs_7_
  415.7 0.1 collective-permute-start.3
  415.9 3.2 collective-permute-start.4
  419.1 0.7 copy-done.14
  419.8 14.8 %shard_map.182 = (bf16[2,768,1792]{2,1,0:T(8,128)(2,1)}, bf16[2,768,1792]{2,1,0:T(8,128)(2,1)}, bf16[2,1792,768]{2,1,0:T(8,128)(2,1)}, f32[2,768,1792]{2,1,0:T(8...) custom-call(s32[1]{0:T(128)} %bitcast.me_ref, ...), custom_call_target="tpu_custom_call", output_to_operand_aliasing={{0}: (19, {}), {1}: (20, {}), {2}: (21, {}), {3}: (22, {}),... | custom-call | flops 12000000000 | bytes 38928384 | tf_op jit(solution)/shard_map/pallas_call | solution.py:486
  434.7 0.6 copy-done.17
  435.3 0.0 copy-done.18
  435.4 0.1 copy-done.19
  435.4 0.1 copy-done.20
  435.5 6.4 %shard_map.183 = (bf16[2,768,1792]{2,1,0:T(8,128)(2,1)}, bf16[2,768,1792]{2,1,0:T(8,128)(2,1)}, bf16[2,1792,768]{2,1,0:T(8,128)(2,1)}, f32[2,768,1792]{2,1,0:T(8...) custom-call(s32[1]{0:T(128)} %bitcast.me_ref, ...), custom_call_target="tpu_custom_call", output_to_operand_aliasing={{0}: (19, {}), {1}: (20, {}), {2}: (21, {}), {3}: (22, {}),... | custom-call | flops 4000000000 | bytes 12976128 | tf_op jit(solution)/shard_map/pallas_call | solution.py:486
  (48 shorter events, 0.1 us)
Async XLA Ops:
  292.4 51.4 %copy-start.1 = (bf16[9,96,256]{2,1,0:T(8,128)(2,1)}, bf16[9,96,256]{2,1,0:T(8,128)(2,1)S(1)}, u32[]{:S(2)}) copy-start(bf16[9,96,256]{2,1,0:T(8,128)(2,1)S(1)} %get-tuple-element.144.refs_0_) | copy-start | bytes 1327108
  292.5 55.5 %copy-start = (bf16[9,96,256]{2,1,0:T(8,128)(2,1)}, bf16[9,96,256]{2,1,0:T(8,128)(2,1)S(1)}, u32[]{:S(2)}) copy-start(bf16[9,96,256]{2,1,0:T(8,128)(2,1)S(1)} %get-tuple-element.199.refs_1_) | copy-start | bytes 1327108
  343.4 27.1 %collective-permute-start.14 = (bf16[9,96,256]{2,1,0:T(8,128)(2,1)S(1)}, bf16[9,96,256]{2,1,0:T(8,128)(2,1)S(1)}, u32[]{:S(2)}, u32[]{:S(2)}) collective-permute-start(bf16[9,96,256]{2,1,0:T(8,128)(2,1)S(1)} %get-tuple-element.144.refs_0_), channel_id=1, source_target_pairs={{0,1},{1,2},{2,3},{3,0},{4,5},{5,6},{6,7},{7,4},{8,9},{9,10},{10,1... | collective-permute-start | bytes 1327112 | tf_op jit(solution)/shard_map/ppermute | solution.py:519
  343.8 29.2 %collective-permute-start.12 = (bf16[9,96,256]{2,1,0:T(8,128)(2,1)S(1)}, bf16[9,96,256]{2,1,0:T(8,128)(2,1)S(1)}, u32[]{:S(2)}, u32[]{:S(2)}) collective-permute-start(bf16[9,96,256]{2,1,0:T(8,128)(2,1)S(1)} %get-tuple-element.144.refs_0_), channel_id=1, source_target_pairs={{0,3},{1,0},{2,1},{3,2},{4,7},{5,4},{6,5},{7,6},{8,11},{9,8},{10,9... | collective-permute-start | bytes 1327112 | tf_op jit(solution)/shard_map/ppermute | solution.py:519
  346.7 27.1 %collective-permute-start.13 = (bf16[9,96,256]{2,1,0:T(8,128)(2,1)S(1)}, bf16[9,96,256]{2,1,0:T(8,128)(2,1)}, u32[]{:S(2)}, u32[]{:S(2)}) collective-permute-start(bf16[9,96,256]{2,1,0:T(8,128)(2,1)S(1)} %get-tuple-element.199.refs_1_), channel_id=1, source_target_pairs={{0,3},{1,0},{2,1},{3,2},{4,7},{5,4},{6,5},{7,6},{8,11},{9,8},{10,9... | collective-permute-start | bytes 1327112 | tf_op jit(solution)/shard_map/ppermute | solution.py:519
  348.0 43.3 %collective-permute-start.17 = (bf16[9,96,256]{2,1,0:T(8,128)(2,1)S(1)}, bf16[9,96,256]{2,1,0:T(8,128)(2,1)}, u32[]{:S(2)}, u32[]{:S(2)}) collective-permute-start(bf16[9,96,256]{2,1,0:T(8,128)(2,1)S(1)} %get-tuple-element.199.refs_1_), channel_id=1, source_target_pairs={{0,1},{1,2},{2,3},{3,0},{4,5},{5,6},{6,7},{7,4},{8,9},{9,10},{10,1... | collective-permute-start | bytes 1327112 | tf_op jit(solution)/shard_map/ppermute | solution.py:519
  349.7 9.9 %copy-start.6 = (bf16[3,96,256]{2,1,0:T(8,128)(2,1)}, bf16[3,96,256]{2,1,0:T(8,128)(2,1)S(1)}, u32[]{:S(2)}) copy-start(bf16[3,96,256]{2,1,0:T(8,128)(2,1)S(1)} %get-tuple-element.204.refs_0_) | copy-start | bytes 442372
  349.7 63.9 %copy-start.5 = (bf16[3,96,256]{2,1,0:T(8,128)(2,1)}, bf16[3,96,256]{2,1,0:T(8,128)(2,1)S(1)}, u32[]{:S(2)}) copy-start(bf16[3,96,256]{2,1,0:T(8,128)(2,1)S(1)} %get-tuple-element.203.refs_1_) | copy-start | bytes 442372
  349.8 19.9 %collective-permute-start.2 = (bf16[3,96,256]{2,1,0:T(8,128)(2,1)S(1)}, bf16[3,96,256]{2,1,0:T(8,128)(2,1)S(1)}, u32[]{:S(2)}, u32[]{:S(2)}) collective-permute-start(bf16[3,96,256]{2,1,0:T(8,128)(2,1)S(1)} %get-tuple-element.204.refs_0_), channel_id=1, source_target_pairs={{0,1},{1,2},{2,3},{3,0},{4,5},{5,6},{6,7},{7,4},{8,9},{9,10},{10,1... | collective-permute-start | bytes 442376 | tf_op jit(solution)/shard_map/ppermute | solution.py:519
  359.7 9.9 %copy-start.4 = (bf16[2,9,96,256]{3,2,1,0:T(8,128)(2,1)S(1)}, bf16[2,9,96,256]{3,2,1,0:T(8,128)(2,1)}, u32[]{:S(2)}) copy-start(bf16[2,9,96,256]{3,2,1,0:T(8,128)(2,1)} %get-tuple-element.141) | copy-start | bytes 2654212
  369.7 21.6 %copy-start.3 = (bf16[9,96,256]{2,1,0:T(8,128)(2,1)}, bf16[9,96,256]{2,1,0:T(8,128)(2,1)S(1)}, u32[]{:S(2)}) copy-start(bf16[9,96,256]{2,1,0:T(8,128)(2,1)S(1)} %get-tuple-element.142.refs_0_) | copy-start | bytes 1327108
  369.7 22.4 %copy-start.2 = (bf16[9,96,256]{2,1,0:T(8,128)(2,1)}, bf16[9,96,256]{2,1,0:T(8,128)(2,1)S(1)}, u32[]{:S(2)}) copy-start(bf16[9,96,256]{2,1,0:T(8,128)(2,1)S(1)} %get-tuple-element.201.refs_1_) | copy-start | bytes 1327108
  369.7 46.0 %copy-start.15 = (bf16[3,96,256]{2,1,0:T(8,128)(2,1)}, bf16[3,96,256]{2,1,0:T(8,128)(2,1)S(1)}, u32[]{:S(2)}) copy-start(bf16[3,96,256]{2,1,0:T(8,128)(2,1)S(1)} %collective-permute-done.2.refs_6_) | copy-start | bytes 442372
  369.7 22.4 %collective-permute-start.8 = (bf16[9,96,256]{2,1,0:T(8,128)(2,1)S(1)}, bf16[9,96,256]{2,1,0:T(8,128)(2,1)S(1)}, u32[]{:S(2)}, u32[]{:S(2)}) collective-permute-start(bf16[9,96,256]{2,1,0:T(8,128)(2,1)S(1)} %get-tuple-element.142.refs_0_), channel_id=1, source_target_pairs={{0,1},{1,2},{2,3},{3,0},{4,5},{5,6},{6,7},{7,4},{8,9},{9,10},{10,1... | collective-permute-start | bytes 1327112 | tf_op jit(solution)/shard_map/ppermute | solution.py:519
  370.4 20.8 %copy-start.8 = (bf16[9,96,256]{2,1,0:T(8,128)(2,1)}, bf16[9,96,256]{2,1,0:T(8,128)(2,1)S(1)}, u32[]{:S(2)}) copy-start(bf16[9,96,256]{2,1,0:T(8,128)(2,1)S(1)} %collective-permute-done.14.refs_6_) | copy-start | bytes 1327108
  370.4 23.1 %collective-permute-start.7 = (bf16[9,96,256]{2,1,0:T(8,128)(2,1)S(1)}, bf16[9,96,256]{2,1,0:T(8,128)(2,1)}, u32[]{:S(2)}, u32[]{:S(2)}) collective-permute-start(bf16[9,96,256]{2,1,0:T(8,128)(2,1)S(1)} %get-tuple-element.201.refs_1_), channel_id=1, source_target_pairs={{0,3},{1,0},{2,1},{3,2},{4,7},{5,4},{6,5},{7,6},{8,11},{9,8},{10,9... | collective-permute-start | bytes 1327112 | tf_op jit(solution)/shard_map/ppermute | solution.py:519
  373.1 18.2 %copy-start.9 = (bf16[9,96,256]{2,1,0:T(8,128)(2,1)}, bf16[9,96,256]{2,1,0:T(8,128)(2,1)S(1)}, u32[]{:S(2)}) copy-start(bf16[9,96,256]{2,1,0:T(8,128)(2,1)S(1)} %collective-permute-done.12.refs_2_) | copy-start | bytes 1327108
  373.1 22.3 %collective-permute-start.15 = (bf16[9,96,256]{2,1,0:T(8,128)(2,1)S(1)}, bf16[9,96,256]{2,1,0:T(8,128)(2,1)}, u32[]{:S(2)}, u32[]{:S(2)}) collective-permute-start(bf16[9,96,256]{2,1,0:T(8,128)(2,1)S(1)} %collective-permute-done.14.refs_6_), channel_id=1, source_target_pairs={{0,1},{1,2},{2,3},{3,0},{4,5},{5,6},{6,7},{7,4},{8,9},{9,10},{10,1... | collective-permute-start | bytes 1327112 | tf_op jit(solution)/shard_map/ppermute | solution.py:519
  373.8 21.8 %collective-permute-start.16 = (bf16[9,96,256]{2,1,0:T(8,128)(2,1)}, bf16[9,96,256]{2,1,0:T(8,128)(2,1)}, u32[]{:S(2)}, u32[]{:S(2)}) collective-permute-start(bf16[9,96,256]{2,1,0:T(8,128)(2,1)} %collective-permute-done.13.refs_3_), channel_id=1, source_target_pairs={{0,3},{1,0},{2,1},{3,2},{4,7},{5,4},{6,5},{7,6},{8,11},{9,8},{10,9... | collective-permute-start | bytes 1327112 | tf_op jit(solution)/shard_map/ppermute | solution.py:519
  391.3 22.4 %collective-permute-start.6 = (bf16[9,96,256]{2,1,0:T(8,128)(2,1)S(1)}, bf16[9,96,256]{2,1,0:T(8,128)(2,1)S(1)}, u32[]{:S(2)}, u32[]{:S(2)}) collective-permute-start(bf16[9,96,256]{2,1,0:T(8,128)(2,1)S(1)} %get-tuple-element.142.refs_0_), channel_id=1, source_target_pairs={{0,3},{1,0},{2,1},{3,2},{4,7},{5,4},{6,5},{7,6},{8,11},{9,8},{10,9... | collective-permute-start | bytes 1327112 | tf_op jit(solution)/shard_map/ppermute | solution.py:519
  392.1 21.4 %copy-start.10 = (bf16[9,96,256]{2,1,0:T(8,128)(2,1)}, bf16[9,96,256]{2,1,0:T(8,128)(2,1)S(1)}, u32[]{:S(2)}) copy-start(bf16[9,96,256]{2,1,0:T(8,128)(2,1)S(1)} %collective-permute-done.8.refs_6_) | copy-start | bytes 1327108
  392.1 23.6 %collective-permute-start.11 = (bf16[9,96,256]{2,1,0:T(8,128)(2,1)S(1)}, bf16[9,96,256]{2,1,0:T(8,128)(2,1)S(1)}, u32[]{:S(2)}, u32[]{:S(2)}) collective-permute-start(bf16[9,96,256]{2,1,0:T(8,128)(2,1)S(1)} %get-tuple-element.201.refs_1_), channel_id=1, source_target_pairs={{0,1},{1,2},{2,3},{3,0},{4,5},{5,6},{6,7},{7,4},{8,9},{9,10},{10,1... | collective-permute-start | bytes 1327112 | tf_op jit(solution)/shard_map/ppermute | solution.py:519
  393.5 20.0 %collective-permute-start.1 = (bf16[3,96,256]{2,1,0:T(8,128)(2,1)S(1)}, bf16[3,96,256]{2,1,0:T(8,128)(2,1)S(1)}, u32[]{:S(2)}, u32[]{:S(2)}) collective-permute-start(bf16[3,96,256]{2,1,0:T(8,128)(2,1)S(1)} %get-tuple-element.203.refs_1_), channel_id=1, source_target_pairs={{0,3},{1,0},{2,1},{3,2},{4,7},{5,4},{6,5},{7,6},{8,11},{9,8},{10,9... | collective-permute-start | bytes 442376 | tf_op jit(solution)/shard_map/ppermute | solution.py:519
  395.4 20.5 %collective-permute-start.9 = (bf16[9,96,256]{2,1,0:T(8,128)(2,1)S(1)}, bf16[9,96,256]{2,1,0:T(8,128)(2,1)S(1)}, u32[]{:S(2)}, u32[]{:S(2)}) collective-permute-start(bf16[9,96,256]{2,1,0:T(8,128)(2,1)S(1)} %collective-permute-done.8.refs_6_), channel_id=1, source_target_pairs={{0,1},{1,2},{2,3},{3,0},{4,5},{5,6},{6,7},{7,4},{8,9},{9,10},{10,1... | collective-permute-start | bytes 1327112 | tf_op jit(solution)/shard_map/ppermute | solution.py:519
  395.5 23.5 %collective-permute-start.10 = (bf16[9,96,256]{2,1,0:T(8,128)(2,1)}, bf16[9,96,256]{2,1,0:T(8,128)(2,1)S(1)}, u32[]{:S(2)}, u32[]{:S(2)}) collective-permute-start(bf16[9,96,256]{2,1,0:T(8,128)(2,1)} %collective-permute-done.7.refs_3_), channel_id=1, source_target_pairs={{0,3},{1,0},{2,1},{3,2},{4,7},{5,4},{6,5},{7,6},{8,11},{9,8},{10,9... | collective-permute-start | bytes 1327112 | tf_op jit(solution)/shard_map/ppermute | solution.py:519
  398.6 14.9 %copy-start.7 = (bf16[3,96,256]{2,1,0:T(8,128)(2,1)S(1)}, bf16[3,96,256]{2,1,0:T(8,128)(2,1)}, u32[]{:S(2)}) copy-start(bf16[3,96,256]{2,1,0:T(8,128)(2,1)} %copy-done.6) | copy-start | bytes 442372
  413.5 21.1 %copy-start.16 = (bf16[3,96,256]{2,1,0:T(8,128)(2,1)}, bf16[3,96,256]{2,1,0:T(8,128)(2,1)S(1)}, u32[]{:S(2)}) copy-start(bf16[3,96,256]{2,1,0:T(8,128)(2,1)S(1)} %collective-permute-done.1.refs_3_) | copy-start | bytes 442372
  413.5 21.1 %collective-permute-start = (bf16[3,96,256]{2,1,0:T(8,128)(2,1)S(1)}, bf16[3,96,256]{2,1,0:T(8,128)(2,1)S(1)}, u32[]{:S(2)}, u32[]{:S(2)}) collective-permute-start(bf16[3,96,256]{2,1,0:T(8,128)(2,1)S(1)} %copy-done.7), channel_id=1, source_target_pairs={{0,3},{1,0},{2,1},{3,2},{4,7},{5,4},{6,5},{7,6},{8,11},{9,8},{10,9... | collective-permute-start | bytes 442376 | tf_op jit(solution)/shard_map/ppermute | solution.py:519
  413.7 5.4 %copy-start.11 = (bf16[9,96,256]{2,1,0:T(8,128)(2,1)}, bf16[9,96,256]{2,1,0:T(8,128)(2,1)S(1)}, u32[]{:S(2)}) copy-start(bf16[9,96,256]{2,1,0:T(8,128)(2,1)S(1)} %collective-permute-done.6.refs_2_) | copy-start | bytes 1327108
  413.7 21.0 %collective-permute-start.5 = (bf16[3,96,256]{2,1,0:T(8,128)(2,1)S(1)}, bf16[3,96,256]{2,1,0:T(8,128)(2,1)S(1)}, u32[]{:S(2)}, u32[]{:S(2)}) collective-permute-start(bf16[3,96,256]{2,1,0:T(8,128)(2,1)S(1)} %get-tuple-element.203.refs_1_), channel_id=1, source_target_pairs={{0,1},{1,2},{2,3},{3,0},{4,5},{5,6},{6,7},{7,4},{8,9},{9,10},{10,1... | collective-permute-start | bytes 442376 | tf_op jit(solution)/shard_map/ppermute | solution.py:519
  415.7 3.3 copy-start.12
  415.7 19.0 %collective-permute-start.3 = (bf16[3,96,256]{2,1,0:T(8,128)(2,1)S(1)}, bf16[3,96,256]{2,1,0:T(8,128)(2,1)S(1)}, u32[]{:S(2)}, u32[]{:S(2)}) collective-permute-start(bf16[3,96,256]{2,1,0:T(8,128)(2,1)S(1)} %collective-permute-done.2.refs_6_), channel_id=1, source_target_pairs={{0,1},{1,2},{2,3},{3,0},{4,5},{5,6},{6,7},{7,4},{8,9},{9,10},{10,1... | collective-permute-start | bytes 442376 | tf_op jit(solution)/shard_map/ppermute | solution.py:519
  415.9 3.2 copy-start.13
  415.9 18.8 %collective-permute-start.4 = (bf16[3,96,256]{2,1,0:T(8,128)(2,1)S(1)}, bf16[3,96,256]{2,1,0:T(8,128)(2,1)S(1)}, u32[]{:S(2)}, u32[]{:S(2)}) collective-permute-start(bf16[3,96,256]{2,1,0:T(8,128)(2,1)S(1)} %collective-permute-done.1.refs_3_), channel_id=1, source_target_pairs={{0,3},{1,0},{2,1},{3,2},{4,7},{5,4},{6,5},{7,6},{8,11},{9,8},{10,9... | collective-permute-start | bytes 442376 | tf_op jit(solution)/shard_map/ppermute | solution.py:519
  419.0 0.8 copy-start.14
  434.7 0.7 copy-start.17
  434.7 0.7 copy-start.18
  434.7 0.7 copy-start.19
  434.7 0.8 copy-start.20

commit v2 on v1

v2 whole, which is shorter than its diff:
```python
import functools

import jax
import jax.numpy as jnp
from jax import lax
from jax.experimental import pallas as pl
from jax.experimental.pallas import tpu as pltpu
from jax.sharding import PartitionSpec as P


F32, BF16 = jnp.float32, jnp.bfloat16
TILE = 512
LONG = 1024
SUB = 512
UNIT = 256
FULL_VMEM = 60 << 20
GROUPS = {1: ((0, 2), (2, 4), (4, 6)), 0: ((0, 3), (3, 6))}


def params(**kw):
    return pltpu.CompilerParams(vmem_limit_bytes=FULL_VMEM, **kw)


def cost(matmuls, moved, tokens, d, width):
    return pl.CostEstimate(flops=2 * matmuls * tokens * d * width, bytes_accessed=moved, transcendentals=0)


def dot(a, b, ca, cb):
    return lax.dot_general(a, b, (((ca,), (cb,)), ((), ())), preferred_element_type=F32)


def scale_of(wide):
    return lax.rsqrt(jnp.mean(wide * wide, -1, keepdims=True) + 1e-6)


def forward_kernel(x_ref, wg_ref, wu_ref, wd_ref, a_ref, h_ref, b_ref, gate_ref, up_ref, p_ref):
    rows = SUB
    for sub in range(x_ref.shape[0] // SUB):
        at = slice(sub * rows, (sub + 1) * rows)
        x = x_ref[at, :].astype(F32)
        a = (x * scale_of(x)).astype(BF16)
        a_ref[at, :] = a
        for j in range(p_ref.shape[1] // UNIT):
            cols = slice(j * UNIT, (j + 1) * UNIT)
            gate = dot(a, wg_ref[:, cols], 1, 0)
            up = dot(a, wu_ref[:, cols], 1, 0)
            gate_ref[at, cols] = gate
            up_ref[at, cols] = up
            p_ref[at, cols] = (gate * jax.nn.sigmoid(gate) * up).astype(BF16)
    for sub in range(x_ref.shape[0] // SUB):
        at = slice(sub * rows, (sub + 1) * rows)
        h = x_ref[at, :] + dot(p_ref[at, :], wd_ref[...], 1, 0).astype(BF16)
        h_ref[at, :] = h
        wide = h.astype(F32)
        b_ref[at, :] = (wide * scale_of(wide)).astype(BF16)


def forward(x, wg, wu, wd, layer):
    tokens, d = x.shape
    ff = wg.shape[2]
    rows = pl.BlockSpec((TILE, d), lambda t: (t, 0))
    hidden = pl.BlockSpec((TILE, ff), lambda t: (t, 0))
    whole = lambda r, c: pl.BlockSpec((None, r, c), lambda t: (layer, 0, 0), pipeline_mode=pl.Buffered(1))
    out = jax.ShapeDtypeStruct((tokens, d), BF16)
    wide = jax.ShapeDtypeStruct((tokens, ff), F32)
    return pl.pallas_call(
        forward_kernel,
        grid=(tokens // TILE,),
        in_specs=[rows, whole(d, ff), whole(d, ff), whole(ff, d)],
        out_specs=[rows] * 3 + [hidden] * 2,
        out_shape=[out] * 3 + [wide] * 2,
        scratch_shapes=[pltpu.VMEM((TILE, ff), BF16)],
        compiler_params=params(dimension_semantics=("arbitrary",)),
        cost_estimate=cost(3, 8 * tokens * d + 6 * d * ff, tokens, d, ff),
        name="forward",
    )(x, wg, wu, wd)


def remote(src, dst, sems, i, to):
    send, recv = sems
    return pltpu.make_async_remote_copy(
        src_ref=src, dst_ref=dst, send_sem=send.at[i], recv_sem=recv.at[i], device_id={"dp": to}, device_id_type=pl.DeviceIdType.MESH
    )


def around(n):
    me = lax.axis_index("dp")
    return lax.rem(me + 1, n), lax.rem(me + n - 1, n)


class Sum:
    def __init__(self, parts, n, middle):
        self.operands, self.n, self.middle = list(parts), n, middle
        half = parts[0].shape[1:]
        self.half = half
        self.outs = [jax.ShapeDtypeStruct(half, BF16)] * 2 + [jax.ShapeDtypeStruct((8, half[-1]), F32)]
        self.out_specs = [pl.BlockSpec(half, lambda t: (0,) * 3)] * 2 + [pl.BlockSpec((8, half[-1]), lambda t: (0, 0))]
        self.scratch = [pltpu.VMEM((k, *half), BF16) for k in (2, 2, 4, 2, 2)]
        self.scratch += [pltpu.SemaphoreType.DMA((6,)), pltpu.SemaphoreType.DMA((6,)), pltpu.SemaphoreType.DMA((1,))]

    def bind(self, refs):
        to_right, to_left, rest, share_a, share_b, self.squares, self.from_left, self.from_right, self.rest, self.sums, self.second, *sems, local = refs
        self.share = share_a, share_b
        right, left = around(self.n)
        self.copies = [
            remote(to_right.at[0], self.from_left.at[0], sems, 0, right),
            remote(to_left.at[0], self.from_right.at[0], sems, 1, left),
            remote(to_right.at[1], self.from_left.at[1], sems, 2, right),
            remote(to_left.at[1], self.from_right.at[1], sems, 3, left),
            remote(self.sums.at[0], self.second.at[0], sems, 4, right),
            remote(self.sums.at[1], self.second.at[1], sems, 5, left),
        ]
        self.local = pltpu.make_async_copy(rest, self.rest, local.at[0])

    def start(self):
        self.local.start()
        for copy in self.copies[:4]:
            copy.start()

    def step(self):
        self.local.wait()
        for i, came in enumerate((self.from_left, self.from_right)):
            self.copies[i].wait_recv()

            @pl.loop(0, self.half[0])
            def _(k):
                self.sums[i, k] = (self.rest[i, k].astype(F32) + came[0, k].astype(F32)).astype(BF16)

            self.copies[4 + i].start()

    def end(self):
        for copy in self.copies[2:]:
            copy.wait_recv()
        self.squares[...] = jnp.zeros_like(self.squares)
        for i, came in enumerate((self.from_right, self.from_left)):

            @pl.loop(0, self.half[0])
            def _(k):
                whole = self.rest[2 + i, k].astype(F32) + came[1, k].astype(F32) + self.second[i, k].astype(F32)
                self.share[i][k] = whole.astype(BF16)
                rounded = whole.astype(BF16).astype(F32)
                self.squares[...] += jnp.sum((rounded * rounded).reshape(-1, 8, rounded.shape[-1]), 0)

        for copy in self.copies:
            copy.wait_send()


def gather_copies(a, b, to, sems, base, n):
    right, left = around(n)
    after_a, after_b, far_a, far_b, before_a, before_b = to
    return [
        remote(a, before_a, sems, base, right),
        remote(b, after_b, sems, base + 1, left),
        remote(b, before_b, sems, base + 2, right),
        remote(a, after_a, sems, base + 3, left),
        remote(before_a, far_a, sems, base + 4, right),
        remote(after_b, far_b, sems, base + 5, left),
    ]


def start_gather(copies):
    for copy in copies[:4]:
        copy.start()


def pass_on(copies):
    for i in range(2):
        copies[i].wait_recv()
        copies[4 + i].start()


def end_gather(copies):
    for copy in copies[2:]:
        copy.wait_recv()
    for copy in copies:
        copy.wait_send()


class Gather:
    def __init__(self, halves, n, middle):
        self.operands, self.n, self.middle = list(halves), n, middle
        self.outs = [jax.ShapeDtypeStruct(halves[0].shape, BF16)] * 6
        self.out_specs = [pl.BlockSpec(memory_space=pl.ANY)] * 6
        self.scratch = [pltpu.SemaphoreType.DMA((6,)), pltpu.SemaphoreType.DMA((6,))]

    def bind(self, refs):
        self.copies = gather_copies(*refs[:2], refs[2:8], refs[8:], 0, self.n)

    def start(self):
        start_gather(self.copies)

    def step(self):
        pass_on(self.copies)

    def end(self):
        end_gather(self.copies)


def run(body, n, steps, ins, in_specs, outs, out_specs, scratch, tasks, number, **kw):
    groups = [(ins, outs, scratch), *((t.operands, t.outs, t.scratch) for t in tasks)]

    def kernel(*refs):
        at, dealt = 0, [[] for _ in groups]
        for which in range(3):
            for i, group in enumerate(groups):
                dealt[i] += refs[at : at + len(group[which])]
                at += len(group[which])
        t = pl.program_id(0)
        for task, own in zip(tasks, dealt[1:], strict=True):
            task.bind(own)
        if tasks:

            @pl.when(t == 0)
            def _():
                barrier = pltpu.get_barrier_semaphore()
                for to in around(n):
                    pl.semaphore_signal(barrier, inc=1, device_id={"dp": to}, device_id_type=pl.DeviceIdType.MESH)
                pl.semaphore_wait(barrier, 2)
                for task in tasks:
                    task.start()

            for task in tasks:
                pl.when(t == task.middle)(task.step)
        body(*dealt[0])
        for task in tasks:
            pl.when(t == steps - 1)(task.end)

    anywhere = pl.BlockSpec(memory_space=pl.ANY)
    out = pl.pallas_call(
        kernel,
        grid=(steps,),
        in_specs=list(in_specs) + [anywhere for t in tasks for _ in t.operands],
        out_specs=list(out_specs) + [s for t in tasks for s in t.out_specs],
        out_shape=list(outs) + [o for t in tasks for o in t.outs],
        scratch_shapes=list(scratch) + [s for t in tasks for s in t.scratch],
        compiler_params=params(
            dimension_semantics=("arbitrary",), **(dict(collective_id=number, has_side_effects=True) if tasks else {})
        ),
        **kw,
    )(*ins, *(o for t in tasks for o in t.operands))
    out, given = list(out), []
    own, out = out[: len(outs)], out[len(outs) :]
    for t in tasks:
        given.append(out[: len(t.outs)])
        out = out[len(t.outs) :]
    return own, *given


def layer_kernel(plan, n, saved, *refs):
    groups, gathers, sources = plan
    refs = list(refs)
    take = lambda k: [refs.pop(0) for _ in range(k)]
    a_ref, dy_ref = take(2)
    gate_ref, up_ref = take(2)
    (wd_ref,) = take(1)
    given = [take(2) for _ in range(sources)]
    last = take(3)
    dgate_ref, dup_ref = take(0 if saved else 2) or (None, None)
    shares = [take(2) for _ in groups]
    (squares,) = take(1)
    places = [take(6) for _ in range(len({g for g, *_ in gathers}))]
    acc, acc_d, p_s = take(3)
    if saved:
        dgate_ref, dup_ref = take(2)
    to_right, to_left, rest, from_left, from_right, sums, second, *sems = refs
    sum_sems, gather_sems = sems[:2], sems[2:]
    p, t = pl.program_id(0), pl.program_id(1)
    parts, steps = pl.num_programs(0), pl.num_programs(1)
    now = p * steps + t
    right, left = around(n)
    _, _, three, part, _ = to_right.shape

    def hops(q):
        base = q * 6
        return [
            remote(to_right.at[q, 0], from_left.at[q, 0], sum_sems, base, right),
            remote(to_left.at[q, 0], from_right.at[q, 0], sum_sems, base + 1, left),
            remote(to_right.at[q, 1], from_left.at[q, 1], sum_sems, base + 2, right),
            remote(to_left.at[q, 1], from_right.at[q, 1], sum_sems, base + 3, left),
            remote(sums.at[q, 0], second.at[q, 0], sum_sems, base + 4, right),
            remote(sums.at[q, 1], second.at[q, 1], sum_sems, base + 5, left),
        ]

    def second_hop(q):
        copies = hops(q)
        for i, came in enumerate((from_left, from_right)):
            copies[i].wait_recv()

            @pl.loop(0, three)
            def _(k):
                sums[q, i, k] = (rest[q, i, k].astype(F32) + came[q, 0, k].astype(F32)).astype(BF16)

            copies[4 + i].start()

    def end_sum(q):
        copies = hops(q)
        for copy in copies[2:]:
            copy.wait_recv()
        for (low, high), share in zip(groups, shares, strict=True):

            @pl.when((q >= low) & (q < high))
            def _():
                for i, came in enumerate((from_right, from_left)):

                    @pl.loop(0, three)
                    def _(k):
                        whole = rest[q, 2 + i, k].astype(F32) + came[q, 1, k].astype(F32) + second[q, i, k].astype(F32)
                        share[i][(q - low) * three + k] = whole.astype(BF16)
                        rounded = whole.astype(BF16).astype(F32)
                        squares[...] += jnp.sum((rounded * rounded).reshape(-1, 8, rounded.shape[-1]), 0)

        for copy in copies:
            copy.wait_send()

    moves = []
    order = sorted({g for g, *_ in gathers})
    for number, (g, unit, first, then) in enumerate(gathers):
        own = given[g - len(groups)] if g >= len(groups) else shares[g]
        rows = pl.ds(unit * three, three)
        to = [ref.at[rows] for ref in places[order.index(g)]]
        moves.append((first, then, gather_copies(own[0].at[rows], own[1].at[rows], to, gather_sems, 6 * number, n)))

    @pl.when(now == 0)
    def _():
        squares[...] = jnp.zeros_like(squares)
        barrier = pltpu.get_barrier_semaphore()
        for to in around(n):
            pl.semaphore_signal(barrier, inc=1, device_id={"dp": to}, device_id_type=pl.DeviceIdType.MESH)
        pl.semaphore_wait(barrier, 2)

    @pl.when((t == 0) & (p > 0))
    def _():
        for copy in hops(p - 1)[:4]:
            copy.start()

    for first, then, copies in moves:
        pl.when(now == first)(functools.partial(start_gather, copies))
        pl.when(now == then)(functools.partial(pass_on, copies))

    @pl.when((t == steps - 1) & (p > 0))
    def _():
        second_hop(p - 1)

    @pl.when((t == steps - 1) & (p > 1))
    def _():
        end_sum(p - 2)

    @pl.when(t == 0)
    def _():
        acc[...] = jnp.zeros_like(acc)
        acc_d[...] = jnp.zeros_like(acc_d)

    def accumulate(at):
        acc[:, :UNIT] += dot(a_ref[at, :], dgate_ref[at, :], 0, 0)
        acc[:, UNIT:] += dot(a_ref[at, :], dup_ref[at, :], 0, 0)
        acc_d[...] += dot(p_s[at, :], dy_ref[at, :], 0, 0)

    spans = [slice(low, low + SUB) for low in range(0, a_ref.shape[0], SUB)]
    for number, at in enumerate(spans):
        gate = gate_ref[at, :] if saved else dot(a_ref[at, :], gate_ref[...], 1, 0)
        up = up_ref[at, :] if saved else dot(a_ref[at, :], up_ref[...], 1, 0)
        dp = dot(dy_ref[at, :], wd_ref[...], 1, 1).astype(BF16).astype(F32)
        s = jax.nn.sigmoid(gate)
        act = gate * s
        p_s[at, :] = (act * up).astype(BF16)
        dup_ref[at, :] = (dp * act).astype(BF16)
        dgate_ref[at, :] = (dp * up * (s * (1.0 + gate * (1.0 - s)))).astype(BF16)
        if number:
            accumulate(spans[number - 1])
    accumulate(spans[-1])

    me = lax.axis_index("dp")
    small = UNIT // (2 * n)

    def put(ref, by, half):
        at = lax.rem(me + by, n) * 2 + half
        rows = pl.ds(pl.multiple_of(at * part, part), part)
        thin = pl.ds(pl.multiple_of(at * small, small), small)
        ref[0] = acc[rows, :UNIT].astype(BF16)
        ref[1] = acc[rows, UNIT:].astype(BF16)
        for b in range(part // small):
            ref[2, b * small : (b + 1) * small, :] = acc_d[thin, b * UNIT : (b + 1) * UNIT].astype(BF16)

    def put_all(to_right, to_left, rest):
        put(to_right.at[0], 2, 0)
        put(to_right.at[1], 1, 1)
        put(to_left.at[0], 2, 1)
        put(to_left.at[1], n - 1, 0)
        put(rest.at[0], 1, 0)
        put(rest.at[1], n - 1, 1)
        put(rest.at[2], 0, 0)
        put(rest.at[3], 0, 1)

    @pl.when((t == steps - 1) & (p < parts - 1))
    def _():
        put_all(to_right.at[p], to_left.at[p], rest.at[p])

    @pl.when((t == steps - 1) & (p == parts - 1))
    def _():
        put_all(*last)
        end_sum(p - 1)
        for _, _, copies in moves:
            end_gather(copies)


def layer_step(a, dy, weights, saved, layer, n, given, gathers, number):
    tokens, d = a.shape
    ff = weights[0].shape[2]
    groups = GROUPS[layer]
    parts, tile, part = ff // UNIT, LONG, d // (2 * n)
    half = (3, part, UNIT)
    rows = pl.BlockSpec((tile, d), lambda p, t: (t, 0))
    cols = pl.BlockSpec((None, d, UNIT), lambda p, t: (layer, 0, p))
    down = pl.BlockSpec((None, UNIT, d), lambda p, t: (layer, p, 0))
    hidden = pl.BlockSpec((tile, UNIT), lambda p, t: (t, p))
    anywhere = pl.BlockSpec(memory_space=pl.ANY)
    const = lambda shape: pl.BlockSpec(shape, lambda p, t: (0,) * len(shape))
    like = lambda shape, dtype=BF16: jax.ShapeDtypeStruct(shape, dtype)
    shapes = [(2, *half), (2, *half), (4, *half)]
    outs = [(like(s), const(s)) for s in shapes]
    if not saved:
        outs += [(like((tokens, ff)), hidden)] * 2
    kept = [(3 * (high - low), part, UNIT) for low, high in groups]
    for s in kept:
        outs += [(like(s), const(s))] * 2
    outs.append((like((8, UNIT), F32), const((8, UNIT))))
    brought = sorted({g for g, *_ in gathers})
    for g in brought:
        s = kept[g] if g < len(groups) else given[g - len(groups)][0].shape
        outs += [(like(s), anywhere)] * 6
    busy = parts - 1
    scratch = [pltpu.VMEM((d, 2 * UNIT), F32), pltpu.VMEM((UNIT, d), F32), pltpu.VMEM((tile, UNIT), BF16)]
    if saved:
        scratch += [pltpu.VMEM((tile, UNIT), BF16)] * 2
    scratch += [pltpu.VMEM((busy, k, *half), BF16) for k in (2, 2, 4, 2, 2, 2, 2)]
    scratch += [pltpu.SemaphoreType.DMA((6 * busy,))] * 2 + [pltpu.SemaphoreType.DMA((6 * len(gathers),))] * 2
    out = pl.pallas_call(
        functools.partial(layer_kernel, (groups, gathers, len(given)), n, bool(saved)),
        grid=(parts, tokens // tile),
        in_specs=[rows, rows] + [hidden if saved else cols] * 2 + [down] + [anywhere] * (2 * len(given)),
        out_specs=[spec for _, spec in outs],
        out_shape=[shape for shape, _ in outs],
        scratch_shapes=scratch,
        compiler_params=params(dimension_semantics=("arbitrary", "arbitrary"), collective_id=number, has_side_effects=True),
        cost_estimate=cost(4 if saved else 6, 4 * tokens * d + 12 * d * ff, tokens, d, ff),
    )(a, dy, *(saved or weights[:2]), weights[2], *(h for g in given for h in g))
    out = list(out)
    take = lambda k: [out.pop(0) for _ in range(k)]
    return take(3), take(0 if saved else 2), [take(2) for _ in groups], take(1)[0], [take(6) for _ in brought]


def back_kernel(dgate_ref, dup_ref, wg_ref, wu_ref, h_ref, dy_ref, out_ref):
    for low in range(0, h_ref.shape[0], SUB):
        span = slice(low, low + SUB)
        by_gate = dot(dgate_ref[span, :], wg_ref[...], 1, 1).astype(BF16)
        da = (by_gate + dot(dup_ref[span, :], wu_ref[...], 1, 1).astype(BF16)).astype(F32)
        h = h_ref[span, :].astype(F32)
        scale = scale_of(h)
        along = jnp.mean(da * h, -1, keepdims=True)
        out_ref[span, :] = dy_ref[span, :] + (da * scale - h * (scale * scale * scale * along)).astype(BF16)


def back(dgate, dup, wg, wu, h, dy, layer, n, tasks=(), number=0):
    tokens, d = h.shape
    ff = wg.shape[2]
    rows = pl.BlockSpec((TILE, d), lambda t: (t, 0))
    whole = pl.BlockSpec((None, d, ff), lambda t: (layer, 0, 0), pipeline_mode=pl.Buffered(1))
    hidden = pl.BlockSpec((TILE, ff), lambda t: (t, 0))
    return run(
        back_kernel,
        n,
        tokens // TILE,
        (dgate, dup, wg, wu, h, dy),
        [hidden, hidden, whole, whole, rows, rows],
        [jax.ShapeDtypeStruct((tokens, d), BF16)],
        [rows],
        (),
        tasks,
        number,
        cost_estimate=cost(2, 6 * tokens * d + 4 * d * ff + 4 * tokens * ff, tokens, d, ff),
        name="back",
    )


class Finish(Sum):
    def __init__(self, parts, n, others, count):
        super().__init__(parts, n, 0)
        self.operands, self.count, self.others = self.operands + list(others), count, len(others)
        tile = (8, others[0].shape[1])
        self.outs.append(jax.ShapeDtypeStruct(tile, F32))
        self.out_specs.append(pl.BlockSpec(tile, lambda t: (0, 0)))
        self.scratch += [pltpu.VMEM((n, *tile), F32), pltpu.VMEM((len(others), *tile), F32), pltpu.SemaphoreType.DMA((1,))]
        self.scratch += [pltpu.SemaphoreType.DMA((n,)), pltpu.SemaphoreType.DMA((n,))]


def finish_kernel(task, refs):
    k = task.others
    parts, others, share, squares, factor = refs[:3], refs[3 : 3 + k], refs[3 + k : 5 + k], refs[5 + k], refs[6 + k]
    rest = refs[7 + k :]
    terms, held, local, send, recv = rest[8:]
    n = task.n
    me = lax.axis_index("dp")
    barrier = pltpu.get_barrier_semaphore()
    for by in range(1, n):
        pl.semaphore_signal(barrier, inc=1, device_id={"dp": lax.rem(me + by, n)}, device_id_type=pl.DeviceIdType.MESH)
    pl.semaphore_wait(barrier, n - 1)
    task.bind([*parts, *share, squares, *rest[:8]])
    task.start()
    for i, other in enumerate(others):
        copy = pltpu.make_async_copy(other, held.at[i], local.at[0])
        copy.start()
        copy.wait()
    task.step()
    task.end()
    total = squares[...]
    for i in range(k):
        total += held[i]
    terms[me] = total
    copies = [remote(terms.at[me], terms.at[me], (send, recv), by, lax.rem(me + by, n)) for by in range(1, n)]
    for copy in copies:
        copy.start()
    for by in range(1, n):
        sender = lax.rem(me + n - by, n)
        remote(terms.at[sender], terms.at[sender], (send, recv), by, lax.rem(me + by, n)).wait_recv()
    everything = terms[0]
    for i in range(1, n):
        everything += terms[i]
    everything = jnp.sum(jnp.sum(everything, 0, keepdims=True), 1, keepdims=True)
    factor[...] = jnp.broadcast_to(jnp.minimum(1.0, 0.5 * lax.rsqrt(everything / task.count + 1e-30)), factor.shape)
    for copy in copies:
        copy.wait_send()


def finish(parts, n, others, count, number):
    task = Finish(parts, n, others, count)
    anywhere = pl.BlockSpec(memory_space=pl.ANY)
    return pl.pallas_call(
        lambda *refs: finish_kernel(task, refs),
        grid=(1,),
        in_specs=[anywhere] * len(task.operands),
        out_specs=task.out_specs,
        out_shape=task.outs,
        scratch_shapes=task.scratch,
        compiler_params=params(collective_id=number, has_side_effects=True),
        cost_estimate=pl.CostEstimate(flops=4 * 10**9, bytes_accessed=10**6, transcendentals=0),
        name="finish",
    )(*task.operands)


def adamw_kernel(n, spans, me_ref, factor_ref, *refs):
    grads, ins, outs = refs[: 2 * n * len(spans)], refs[2 * n * len(spans) :][:9], refs[-9:]
    factor = factor_ref[0:1, 0:1]
    me = me_ref[0]

    def take(grads):
        for number, ref in enumerate(grads):
            at = lax.rem(me + number // 2, n) * 2 + number % 2
            part = ref.shape[1]
            for which in range(3):
                w_ref, m_ref, v_ref = (ins[which + 3 * i] for i in range(3))
                w_out, m_out, v_out = (outs[which + 3 * i] for i in range(3))
                if which < 2:
                    spots = [((pl.ds(pl.multiple_of(at * part, part), part), slice(None)), ref[which])]
                else:
                    small = w_ref.shape[0] // (2 * n)
                    rows = pl.ds(pl.multiple_of(at * small, small), small)
                    spots = [((rows, slice(b * UNIT, (b + 1) * UNIT)), ref[which, b * small : (b + 1) * small]) for b in range(part // small)]
                for spot, g in spots:
                    g = g.astype(F32) * factor
                    m = 0.9 * m_ref[spot] + 0.1 * g
                    v = 0.95 * v_ref[spot] + 0.05 * g * g
                    w = w_ref[spot].astype(F32)
                    m_out[spot] = m
                    v_out[spot] = v
                    w_out[spot] = (w - 0.02 * (m * lax.rsqrt(v + 1e-8) + 0.1 * w)).astype(BF16)

    s = pl.program_id(0)
    for i, (low, high) in enumerate(spans):
        pl.when((s >= low) & (s < high))(functools.partial(take, grads[2 * n * i : 2 * n * (i + 1)]))


def adamw(arrays, done, groups, me, factor, layer, start, n):
    d = arrays[0].shape[1]
    ends = [0]
    for group in groups:
        ends.append(ends[-1] + group[0].shape[0] // 3)
    spans = list(zip(ends, ends[1:]))
    wide = pl.BlockSpec((None, d, UNIT), lambda s, me: (layer, 0, start + s))
    tall = pl.BlockSpec((None, UNIT, d), lambda s, me: (layer, start + s, 0))
    specs = [wide, wide, tall] * 3
    grad = lambda low, high, g: pl.BlockSpec((3,) + g.shape[1:], lambda s, me: (jnp.clip(s - low, 0, high - low - 1), 0, 0))
    grads = [(g, grad(*span, g)) for group, span in zip(groups, spans, strict=True) for g in group]
    held = [] if done is None else list(done)
    return pl.pallas_call(
        functools.partial(adamw_kernel, n, spans),
        grid_spec=pltpu.PrefetchScalarGridSpec(
            num_scalar_prefetch=1,
            grid=(ends[-1],),
            in_specs=[pl.BlockSpec(factor.shape, lambda s, me: (0, 0))]
            + [spec for _, spec in grads]
            + specs
            + [pl.BlockSpec(memory_space=pl.ANY)] * len(held),
            out_specs=specs,
        ),
        out_shape=[jax.ShapeDtypeStruct(a.shape, a.dtype) for a in arrays],
        input_output_aliases={2 + len(grads) + 9 + i: i for i in range(len(held))},
        compiler_params=params(dimension_semantics=("arbitrary",)),
        cost_estimate=pl.CostEstimate(flops=10**9 * 4 * ends[-1], bytes_accessed=22 * 3 * ends[-1] * UNIT * d, transcendentals=0),
    )(me[None], factor, *(g for g, _ in grads), *arrays, *held)


def tie(value, *others):
    return lax.optimization_barrier((value, *others))[0]


def solution(mesh):
    n = mesh.shape["dp"]

    def step(x, dy, *arrays):
        weights = arrays[:3]
        wg, wu, wd = weights
        x, dy = x[0], dy[0]
        me = lax.axis_index("dp")
        count = sum(a.size for a in weights)

        def send(array, by):
            return lax.ppermute(array, "dp", [(i, (i + by) % n) for i in range(n)])

        def spread(a, b):
            ra, lb = send(a, 1), send(b, -1)
            rb, la = send(b, 1), send(a, -1)
            return a, b, la, lb, ra, rb

        def onward(got):
            a, b, la, lb, ra, rb = got
            return a, b, la, lb, send(ra, 1), send(lb, -1), ra, rb

        a0, h1, a1, gate, up = forward(x, wg, wu, wd, 0)
        last, by_hidden, shares, squares, (first,) = layer_step(a1, dy, weights, (), 1, n, (), ((0, 0, 13, 17), (0, 1, 17, 21)), 1)
        tasks = [Sum(last, n, 2), Gather(shares[1], n, 4)]
        (by_h,), own, second = back(*by_hidden, wg, wu, h1, dy, 1, n, tasks, 2)
        own, fresh = own[:2], own[2]
        waiting = ((2, 0, 0, 3), (2, 1, 1, 5), (3, 0, 2, 7))
        last, _, ours, sums, (third, fourth) = layer_step(a0, by_h, weights, (gate, up), 0, n, (shares[2], own), waiting, 3)
        sa, sb, _, factor = finish(last, n, (squares, fresh, sums), count, 4)

        got = [spread(*[tie(h, factor) for h in ours[0]]), spread(*[tie(h, factor) for h in ours[1]]), spread(sa, sb)]
        one = [(*shares[0], *first), (*shares[1], *second), (*shares[2], *third), (*own, *fourth)]
        step_on = lambda done, groups, layer, start: adamw(arrays, done, groups, me, factor, layer, start, n)
        done = step_on(None, one[:2], 1, 0)
        done = step_on(done, one[2:], 1, GROUPS[1][2][0])
        done = step_on(done, [onward(got[0])], 0, 0)
        done = step_on(done, [onward(got[2])], 0, GROUPS[0][-1][1])
        done = step_on(done, [onward(got[1])], 0, GROUPS[0][1][0])
        return tuple(done)

    return jax.shard_map(
        step,
        mesh=mesh,
        in_specs=(P(("rep", "dp"), None, None),) * 2 + (P(None, None, None),) * 9,
        out_specs=(P("rep", None, None),) * 9,
        check_vma=False,
    )
```

time: 450 us -> 402 us (0.89); the launches traced: 442 us -> 402 us
  Pallas kernels: 412 us -> 373 us
  waiting for transfers between devices: 0.05 us -> 7.95 us
  starting transfers between devices: 24.9 us -> 18.4 us
    pallas_call x7 -> x1, Pallas kernels: 279 us -> 37.6 us  [run(): pl.pallas_call(kernel, grid=(steps,), in_specs=list(in_specs) + [anywhere...]
    pallas_call x6 -> x7, Pallas kernels: 70.7 us -> 273 us  [the longest x2 199 us: layer_step(): pl.pallas_call(functools.partial(layer_kernel, (groups, gathers, len(give...]
    ppermute x18, waiting for transfers between devices: 0.05 us -> 7.95 us  [send(): return lax.ppermute(array, 'dp', [(i, (i + by) % n) for i in range(n)])]
    ppermute x18, starting transfers between devices: 24.9 us -> 18.4 us  [send(): return lax.ppermute(array, 'dp', [(i, (i + by) % n) for i in range(n)])]
  transfers between devices with their start and end apart: 18 -> 18, of which waited for: 0 -> 3; matrix products, arithmetic and copies ran while one was open for 0% -> 0% of each run, Pallas kernels for 15% -> 14%
where the time goes in v2:
time: 402 us
  Pallas kernels  373 us (93%)
  starting transfers between devices  18.4 us (5%)
  waiting for transfers between devices  7.95 us (2%)
    pallas_call x2, Pallas kernels, layer_step(): pl.pallas_call(functools.partial(layer_kernel, (groups, gathers, len(give...  199 us
    pallas_call x5, Pallas kernels, adamw(): pl.pallas_call(functools.partial(adamw_kernel, n, spans), grid_spec=pltpu...  73.5 us
    pallas_call x1, Pallas kernels, forward(): pl.pallas_call(forward_kernel, grid=(tokens // TILE,), in_specs=[rows, wh...  45.9 us
    pallas_call x1, Pallas kernels, run(): pl.pallas_call(kernel, grid=(steps,), in_specs=list(in_specs) + [anywhere...  37.6 us
    ppermute x18, starting transfers between devices, send(): return lax.ppermute(array, 'dp', [(i, (i + by) % n) for i in range(n)])  18.4 us
    pallas_call x1, Pallas kernels, finish(): pl.pallas_call(lambda *refs: finish_kernel(task, refs), grid=(1,), in_spe...  16.2 us
  transfers between devices with their start and end apart: 18, of which 3 were waited for; matrix products, arithmetic and copies ran while one was open for 0% of the time, Pallas kernels for 14%

profile of v2, /device:TPU:112, one launch (start us, length us, event | category | flops | bytes accessed | tf_op | source)
XLA Modules:
  0.0 401.8 jit_solution(8919236150203359156)
XLA Ops:
  0.6 45.9 %forward.1 = (bf16[4096,768]{1,0:T(8,128)(2,1)}, bf16[4096,768]{1,0:T(8,128)(2,1)}, bf16[4096,768]{1,0:T(8,128)(2,1)}, f32[4096,1792]{1,0:T(8,128)}, f32[4096,1792]{1,0:T(8,128)}) custom-call(bf16[4096,768]{1,0:T(8,128)(2,1)} %bitcast.3, bf16[2,768,1792]{2,1,0:T(8,128)(2,1)} %refs_8_.5, bf16[2,768,1792]{2,1,0:T(8,128)(2,1)} %refs_9_.5, ...), custom_call_target="tpu_custom_call" | custom-call | flops 33822867456 | bytes 33423360 | tf_op jit(solution)/shard_map/forward/pallas_call | solution.py:66
  46.5 102.8 %shard_map.178 = (bf16[2,3,96,256]{3,2,1,0:T(8,128)(2,1)}, bf16[2,3,96,256]{3,2,1,0:T(8,128)(2,1)}, bf16[4,3,96,256]{3,2,1,0:T(8,128)(2,1)}, bf16[4096,1792]{1,0...) custom-call(bf16[4096,768]{1,0:T(8,128)(2,1)} %get-tuple-element.106, ...), custom_call_target="tpu_custom_call" | custom-call | flops 67645734912 | bytes 29097984 | tf_op jit(solution)/shard_map/pallas_call | solution.py:437
  149.3 37.6 %back.1 = (bf16[4096,768]{1,0:T(8,128)(2,1)}, bf16[3,96,256]{2,1,0:T(8,128)(2,1)}, bf16[3,96,256]{2,1,0:T(8,128)(2,1)}, f32[8,256]{1,0:T(8,128)}, bf16[6,96,256]...) custom-call(bf16[4096,1792]{1,0:T(8,128)(2,1)} %get-tuple-element.10, ...), custom_call_target="tpu_custom_call" | custom-call | flops 22548578304 | bytes 53739520 | tf_op jit(solution)/shard_map/back/pallas_call | solution.py:229
  186.9 96.5 %shard_map.179 = (bf16[2,3,96,256]{3,2,1,0:T(8,128)(2,1)}, bf16[2,3,96,256]{3,2,1,0:T(8,128)(2,1)}, bf16[4,3,96,256]{3,2,1,0:T(8,128)(2,1)}, bf16[9,96,256]{2,1,...) custom-call(bf16[4096,768]{1,0:T(8,128)(2,1)} %get-tuple-element.105, ...), custom_call_target="tpu_custom_call" | custom-call | flops 45097156608 | bytes 29097984 | tf_op jit(solution)/shard_map/pallas_call | solution.py:437
  283.5 16.2 %finish.1 = (bf16[3,96,256]{2,1,0:T(8,128)(2,1)}, bf16[3,96,256]{2,1,0:T(8,128)(2,1)}, f32[8,256]{1,0:T(8,128)}, f32[8,256]{1,0:T(8,128)}) custom-call(bf16[2,3,96,256]{3,2,1,0:T(8,128)(2,1)} %get-tuple-element.122.refs_0_, bf16[2,3,96,256]{3,2,1,0:T(8,128)(2,1)} %get-tuple-element.123.refs_1_, bf16[4,3,96,256]{3,2,1,0:T(8,128)(2,1)} %get-tuple-element.124.refs_2_, ...), custom_call_target="tpu_custom_call" | custom-call | flops 4000000000 | bytes 1000000 | tf_op jit(solution)/shard_map/finish/pallas_call | solution.py:537
  299.7 1.4 collective-permute-start.7
  301.1 0.7 collective-permute-start.8
  301.8 0.8 collective-permute-start.11
  302.6 2.4 collective-permute-start.13
  305.0 0.0 collective-permute-start.17
  305.0 1.7 collective-permute-done.7.refs_3_
  306.7 2.5 collective-permute-start.6
  309.2 0.0 collective-permute-done.8.refs_6_
  309.2 0.1 collective-permute-start.14
  309.3 3.0 collective-permute-done.11.refs_7_
  312.4 0.2 collective-permute-start.10
  312.5 0.5 copy-done.16
  313.0 18.2 %shard_map.180 = (bf16[2,768,1792]{2,1,0:T(8,128)(2,1)}, bf16[2,768,1792]{2,1,0:T(8,128)(2,1)}, bf16[2,1792,768]{2,1,0:T(8,128)(2,1)}, f32[2,768,1792]{2,1,0:T(8...) custom-call(s32[1]{0:T(128)} %bitcast.me_ref, ...), custom_call_target="tpu_custom_call" | custom-call | flops 16000000000 | bytes 51904512 | tf_op jit(solution)/shard_map/pallas_call | solution.py:594
  331.2 0.0 collective-permute-done.6.refs_2_
  331.2 0.4 collective-permute-start.12
  331.7 0.2 copy-done.17
  331.9 1.1 collective-permute-start.1
  333.0 0.0 collective-permute-done.13.refs_3_
  333.0 1.0 collective-permute-start.2
  334.0 2.3 collective-permute-start.16
  336.3 0.0 collective-permute-done.17.refs_7_
  336.3 0.0 collective-permute-start.15
  336.3 16.5 %shard_map.181 = (bf16[2,768,1792]{2,1,0:T(8,128)(2,1)}, bf16[2,768,1792]{2,1,0:T(8,128)(2,1)}, bf16[2,1792,768]{2,1,0:T(8,128)(2,1)}, f32[2,768,1792]{2,1,0:T(8...) custom-call(s32[1]{0:T(128)} %bitcast.me_ref, ...), custom_call_target="tpu_custom_call", output_to_operand_aliasing={{0}: (27, {}), {1}: (28, {}), {2}: (29, {}), {3}: (30, {}),... | custom-call | flops 12000000000 | bytes 38928384 | tf_op jit(solution)/shard_map/pallas_call | solution.py:594
  352.9 0.0 collective-permute-done.12.refs_2_
  352.9 1.2 collective-permute-start.5
  354.1 0.0 collective-permute-done.1.refs_3_
  354.1 2.1 collective-permute-start
  356.2 0.0 collective-permute-done.2.refs_6_
  356.2 0.1 collective-permute-start.9
  356.3 3.2 collective-permute-done.16.refs_5_
  359.5 0.5 collective-permute-start.4
  360.0 0.0 collective-permute-done.15.refs_4_
  360.0 1.5 collective-permute-start.3
  361.5 16.2 %shard_map.182 = (bf16[2,768,1792]{2,1,0:T(8,128)(2,1)}, bf16[2,768,1792]{2,1,0:T(8,128)(2,1)}, bf16[2,1792,768]{2,1,0:T(8,128)(2,1)}, f32[2,768,1792]{2,1,0:T(8...) custom-call(s32[1]{0:T(128)} %bitcast.me_ref, ...), custom_call_target="tpu_custom_call", output_to_operand_aliasing={{0}: (19, {}), {1}: (20, {}), {2}: (21, {}), {3}: (22, {}),... | custom-call | flops 12000000000 | bytes 38928384 | tf_op jit(solution)/shard_map/pallas_call | solution.py:594
  377.8 6.5 %shard_map.183 = (bf16[2,768,1792]{2,1,0:T(8,128)(2,1)}, bf16[2,768,1792]{2,1,0:T(8,128)(2,1)}, bf16[2,1792,768]{2,1,0:T(8,128)(2,1)}, f32[2,768,1792]{2,1,0:T(8...) custom-call(s32[1]{0:T(128)} %bitcast.me_ref, ...), custom_call_target="tpu_custom_call", output_to_operand_aliasing={{0}: (19, {}), {1}: (20, {}), {2}: (21, {}), {3}: (22, {}),... | custom-call | flops 4000000000 | bytes 12976128 | tf_op jit(solution)/shard_map/pallas_call | solution.py:594
  384.3 0.0 collective-permute-done.5.refs_7_
  384.3 0.0 collective-permute-done.refs_2_
  384.3 0.0 collective-permute-done.3.refs_4_
  384.3 0.7 copy-done.9
  385.0 0.2 copy-done.10
  385.2 0.1 copy-done.11
  385.3 0.1 copy-done.12
  385.5 16.2 %shard_map.184 = (bf16[2,768,1792]{2,1,0:T(8,128)(2,1)}, bf16[2,768,1792]{2,1,0:T(8,128)(2,1)}, bf16[2,1792,768]{2,1,0:T(8,128)(2,1)}, f32[2,768,1792]{2,1,0:T(8...) custom-call(s32[1]{0:T(128)} %bitcast.me_ref, ...), custom_call_target="tpu_custom_call", output_to_operand_aliasing={{0}: (19, {}), {1}: (20, {}), {2}: (21, {}), {3}: (22, {}),... | custom-call | flops 12000000000 | bytes 38928384 | tf_op jit(solution)/shard_map/pallas_call | solution.py:594
  (34 shorter events, 0.1 us)
Async XLA Ops:
  283.4 19.1 %copy-start.3 = (bf16[9,96,256]{2,1,0:T(8,128)(2,1)S(1)}, bf16[9,96,256]{2,1,0:T(8,128)(2,1)}, u32[]{:S(2)}) copy-start(bf16[9,96,256]{2,1,0:T(8,128)(2,1)} %get-tuple-element.138.refs_1_) | copy-start | bytes 1327108
  283.4 25.8 %copy-start.2 = (bf16[9,96,256]{2,1,0:T(8,128)(2,1)S(1)}, bf16[9,96,256]{2,1,0:T(8,128)(2,1)}, u32[]{:S(2)}) copy-start(bf16[9,96,256]{2,1,0:T(8,128)(2,1)} %get-tuple-element.136.refs_0_) | copy-start | bytes 1327108
  299.7 7.0 %collective-permute-start.7 = (bf16[3,96,256]{2,1,0:T(8,128)(2,1)}, bf16[3,96,256]{2,1,0:T(8,128)(2,1)S(1)}, u32[]{:S(2)}, u32[]{:S(2)}) collective-permute-start(bf16[3,96,256]{2,1,0:T(8,128)(2,1)} %get-tuple-element.134.refs_1_), channel_id=1, source_target_pairs={{0,3},{1,0},{2,1},{3,2},{4,7},{5,4},{6,5},{7,6},{8,11},{9,8},{10,9... | collective-permute-start | bytes 442376 | tf_op jit(solution)/shard_map/ppermute | solution.py:627
  301.1 8.1 %collective-permute-start.8 = (bf16[3,96,256]{2,1,0:T(8,128)(2,1)}, bf16[3,96,256]{2,1,0:T(8,128)(2,1)S(1)}, u32[]{:S(2)}, u32[]{:S(2)}) collective-permute-start(bf16[3,96,256]{2,1,0:T(8,128)(2,1)} %get-tuple-element.133.refs_0_), channel_id=1, source_target_pairs={{0,1},{1,2},{2,3},{3,0},{4,5},{5,6},{6,7},{7,4},{8,9},{9,10},{10,1... | collective-permute-start | bytes 442376 | tf_op jit(solution)/shard_map/ppermute | solution.py:627
  301.8 10.6 %collective-permute-start.11 = (bf16[3,96,256]{2,1,0:T(8,128)(2,1)}, bf16[3,96,256]{2,1,0:T(8,128)(2,1)S(1)}, u32[]{:S(2)}, u32[]{:S(2)}) collective-permute-start(bf16[3,96,256]{2,1,0:T(8,128)(2,1)} %get-tuple-element.134.refs_1_), channel_id=1, source_target_pairs={{0,1},{1,2},{2,3},{3,0},{4,5},{5,6},{6,7},{7,4},{8,9},{9,10},{10,1... | collective-permute-start | bytes 442376 | tf_op jit(solution)/shard_map/ppermute | solution.py:627
  302.6 30.4 %collective-permute-start.13 = (bf16[9,96,256]{2,1,0:T(8,128)(2,1)S(1)}, bf16[9,96,256]{2,1,0:T(8,128)(2,1)S(1)}, u32[]{:S(2)}, u32[]{:S(2)}) collective-permute-start(bf16[9,96,256]{2,1,0:T(8,128)(2,1)S(1)} %copy-done.3), channel_id=1, source_target_pairs={{0,3},{1,0},{2,1},{3,2},{4,7},{5,4},{6,5},{7,6},{8,11},{9,8},{10,9... | collective-permute-start | bytes 1327112 | tf_op jit(solution)/shard_map/ppermute | solution.py:627
  305.0 31.3 %collective-permute-start.17 = (bf16[9,96,256]{2,1,0:T(8,128)(2,1)S(1)}, bf16[9,96,256]{2,1,0:T(8,128)(2,1)S(1)}, u32[]{:S(2)}, u32[]{:S(2)}) collective-permute-start(bf16[9,96,256]{2,1,0:T(8,128)(2,1)S(1)} %copy-done.3), channel_id=1, source_target_pairs={{0,1},{1,2},{2,3},{3,0},{4,5},{5,6},{6,7},{7,4},{8,9},{9,10},{10,1... | collective-permute-start | bytes 1327112 | tf_op jit(solution)/shard_map/ppermute | solution.py:627
  306.7 24.6 %copy-start.13 = (bf16[3,96,256]{2,1,0:T(8,128)(2,1)}, bf16[3,96,256]{2,1,0:T(8,128)(2,1)S(1)}, u32[]{:S(2)}) copy-start(bf16[3,96,256]{2,1,0:T(8,128)(2,1)S(1)} %collective-permute-done.7.refs_3_) | copy-start | bytes 442372
  306.7 24.6 %collective-permute-start.6 = (bf16[3,96,256]{2,1,0:T(8,128)(2,1)}, bf16[3,96,256]{2,1,0:T(8,128)(2,1)S(1)}, u32[]{:S(2)}, u32[]{:S(2)}) collective-permute-start(bf16[3,96,256]{2,1,0:T(8,128)(2,1)} %get-tuple-element.133.refs_0_), channel_id=1, source_target_pairs={{0,3},{1,0},{2,1},{3,2},{4,7},{5,4},{6,5},{7,6},{8,11},{9,8},{10,9... | collective-permute-start | bytes 442376 | tf_op jit(solution)/shard_map/ppermute | solution.py:627
  309.2 3.3 copy-start.14
  309.2 24.8 %collective-permute-start.14 = (bf16[9,96,256]{2,1,0:T(8,128)(2,1)S(1)}, bf16[9,96,256]{2,1,0:T(8,128)(2,1)S(1)}, u32[]{:S(2)}, u32[]{:S(2)}) collective-permute-start(bf16[9,96,256]{2,1,0:T(8,128)(2,1)S(1)} %copy-done.2), channel_id=1, source_target_pairs={{0,1},{1,2},{2,3},{3,0},{4,5},{5,6},{6,7},{7,4},{8,9},{9,10},{10,1... | collective-permute-start | bytes 1327112 | tf_op jit(solution)/shard_map/ppermute | solution.py:627
  312.4 0.7 copy-start.16
  312.4 19.5 %collective-permute-start.10 = (bf16[3,96,256]{2,1,0:T(8,128)(2,1)S(1)}, bf16[3,96,256]{2,1,0:T(8,128)(2,1)}, u32[]{:S(2)}, u32[]{:S(2)}) collective-permute-start(bf16[3,96,256]{2,1,0:T(8,128)(2,1)S(1)} %collective-permute-done.7.refs_3_), channel_id=1, source_target_pairs={{0,3},{1,0},{2,1},{3,2},{4,7},{5,4},{6,5},{7,6},{8,11},{9,8},{10,9... | collective-permute-start | bytes 442376 | tf_op jit(solution)/shard_map/ppermute | solution.py:627
  313.0 18.9 %copy-start.1 = (bf16[9,96,256]{2,1,0:T(8,128)(2,1)S(1)}, bf16[9,96,256]{2,1,0:T(8,128)(2,1)}, u32[]{:S(2)}) copy-start(bf16[9,96,256]{2,1,0:T(8,128)(2,1)} %get-tuple-element.132.refs_1_) | copy-start | bytes 1327108
  313.0 20.0 %copy-start = (bf16[9,96,256]{2,1,0:T(8,128)(2,1)S(1)}, bf16[9,96,256]{2,1,0:T(8,128)(2,1)}, u32[]{:S(2)}) copy-start(bf16[9,96,256]{2,1,0:T(8,128)(2,1)} %get-tuple-element.130.refs_0_) | copy-start | bytes 1327108
  331.2 0.7 copy-start.17
  331.2 21.6 %collective-permute-start.12 = (bf16[9,96,256]{2,1,0:T(8,128)(2,1)S(1)}, bf16[9,96,256]{2,1,0:T(8,128)(2,1)}, u32[]{:S(2)}, u32[]{:S(2)}) collective-permute-start(bf16[9,96,256]{2,1,0:T(8,128)(2,1)S(1)} %copy-done.2), channel_id=1, source_target_pairs={{0,3},{1,0},{2,1},{3,2},{4,7},{5,4},{6,5},{7,6},{8,11},{9,8},{10,9... | collective-permute-start | bytes 1327112 | tf_op jit(solution)/shard_map/ppermute | solution.py:627
  331.9 22.2 %collective-permute-start.1 = (bf16[9,96,256]{2,1,0:T(8,128)(2,1)S(1)}, bf16[9,96,256]{2,1,0:T(8,128)(2,1)S(1)}, u32[]{:S(2)}, u32[]{:S(2)}) collective-permute-start(bf16[9,96,256]{2,1,0:T(8,128)(2,1)S(1)} %copy-done.1), channel_id=1, source_target_pairs={{0,3},{1,0},{2,1},{3,2},{4,7},{5,4},{6,5},{7,6},{8,11},{9,8},{10,9... | collective-permute-start | bytes 1327112 | tf_op jit(solution)/shard_map/ppermute | solution.py:627
  333.0 19.9 %copy-start.4 = (bf16[9,96,256]{2,1,0:T(8,128)(2,1)}, bf16[9,96,256]{2,1,0:T(8,128)(2,1)S(1)}, u32[]{:S(2)}) copy-start(bf16[9,96,256]{2,1,0:T(8,128)(2,1)S(1)} %collective-permute-done.13.refs_3_) | copy-start | bytes 1327108
  333.0 23.2 %collective-permute-start.2 = (bf16[9,96,256]{2,1,0:T(8,128)(2,1)S(1)}, bf16[9,96,256]{2,1,0:T(8,128)(2,1)S(1)}, u32[]{:S(2)}, u32[]{:S(2)}) collective-permute-start(bf16[9,96,256]{2,1,0:T(8,128)(2,1)S(1)} %copy-done), channel_id=1, source_target_pairs={{0,1},{1,2},{2,3},{3,0},{4,5},{5,6},{6,7},{7,4},{8,9},{9,10},{10,1... | collective-permute-start | bytes 1327112 | tf_op jit(solution)/shard_map/ppermute | solution.py:627
  334.0 18.8 %copy-start.8 = (bf16[9,96,256]{2,1,0:T(8,128)(2,1)}, bf16[9,96,256]{2,1,0:T(8,128)(2,1)S(1)}, u32[]{:S(2)}) copy-start(bf16[9,96,256]{2,1,0:T(8,128)(2,1)S(1)} %collective-permute-done.14.refs_6_) | copy-start | bytes 1327108
  334.0 25.5 %collective-permute-start.16 = (bf16[9,96,256]{2,1,0:T(8,128)(2,1)S(1)}, bf16[9,96,256]{2,1,0:T(8,128)(2,1)}, u32[]{:S(2)}, u32[]{:S(2)}) collective-permute-start(bf16[9,96,256]{2,1,0:T(8,128)(2,1)S(1)} %collective-permute-done.13.refs_3_), channel_id=1, source_target_pairs={{0,3},{1,0},{2,1},{3,2},{4,7},{5,4},{6,5},{7,6},{8,11},{9,8},{10,9... | collective-permute-start | bytes 1327112 | tf_op jit(solution)/shard_map/ppermute | solution.py:627
  336.3 16.6 %copy-start.6 = (bf16[9,96,256]{2,1,0:T(8,128)(2,1)}, bf16[9,96,256]{2,1,0:T(8,128)(2,1)S(1)}, u32[]{:S(2)}) copy-start(bf16[9,96,256]{2,1,0:T(8,128)(2,1)S(1)} %collective-permute-done.17.refs_7_) | copy-start | bytes 1327108
  336.3 23.7 %collective-permute-start.15 = (bf16[9,96,256]{2,1,0:T(8,128)(2,1)S(1)}, bf16[9,96,256]{2,1,0:T(8,128)(2,1)}, u32[]{:S(2)}, u32[]{:S(2)}) collective-permute-start(bf16[9,96,256]{2,1,0:T(8,128)(2,1)S(1)} %collective-permute-done.14.refs_6_), channel_id=1, source_target_pairs={{0,1},{1,2},{2,3},{3,0},{4,5},{5,6},{6,7},{7,4},{8,9},{9,10},{10,1... | collective-permute-start | bytes 1327112 | tf_op jit(solution)/shard_map/ppermute | solution.py:627
  336.3 19.9 %copy-start.15 = (bf16[3,96,256]{2,1,0:T(8,128)(2,1)S(1)}, bf16[3,96,256]{2,1,0:T(8,128)(2,1)}, u32[]{:S(2)}) copy-start(bf16[3,96,256]{2,1,0:T(8,128)(2,1)} %copy-done.14) | copy-start | bytes 442372
  352.9 31.4 %collective-permute-start.5 = (bf16[9,96,256]{2,1,0:T(8,128)(2,1)S(1)}, bf16[9,96,256]{2,1,0:T(8,128)(2,1)S(1)}, u32[]{:S(2)}, u32[]{:S(2)}) collective-permute-start(bf16[9,96,256]{2,1,0:T(8,128)(2,1)S(1)} %copy-done.1), channel_id=1, source_target_pairs={{0,1},{1,2},{2,3},{3,0},{4,5},{5,6},{6,7},{7,4},{8,9},{9,10},{10,1... | collective-permute-start | bytes 1327112 | tf_op jit(solution)/shard_map/ppermute | solution.py:627
  354.1 23.6 %copy-start.5 = (bf16[9,96,256]{2,1,0:T(8,128)(2,1)}, bf16[9,96,256]{2,1,0:T(8,128)(2,1)S(1)}, u32[]{:S(2)}) copy-start(bf16[9,96,256]{2,1,0:T(8,128)(2,1)S(1)} %collective-permute-done.1.refs_3_) | copy-start | bytes 1327108
  354.1 30.1 %collective-permute-start = (bf16[9,96,256]{2,1,0:T(8,128)(2,1)S(1)}, bf16[9,96,256]{2,1,0:T(8,128)(2,1)S(1)}, u32[]{:S(2)}, u32[]{:S(2)}) collective-permute-start(bf16[9,96,256]{2,1,0:T(8,128)(2,1)S(1)} %copy-done), channel_id=1, source_target_pairs={{0,3},{1,0},{2,1},{3,2},{4,7},{5,4},{6,5},{7,6},{8,11},{9,8},{10,9... | collective-permute-start | bytes 1327112 | tf_op jit(solution)/shard_map/ppermute | solution.py:627
  356.2 21.5 %copy-start.7 = (bf16[9,96,256]{2,1,0:T(8,128)(2,1)}, bf16[9,96,256]{2,1,0:T(8,128)(2,1)S(1)}, u32[]{:S(2)}) copy-start(bf16[9,96,256]{2,1,0:T(8,128)(2,1)S(1)} %collective-permute-done.2.refs_6_) | copy-start | bytes 1327108
  356.2 21.5 %collective-permute-start.9 = (bf16[3,96,256]{2,1,0:T(8,128)(2,1)S(1)}, bf16[3,96,256]{2,1,0:T(8,128)(2,1)}, u32[]{:S(2)}, u32[]{:S(2)}) collective-permute-start(bf16[3,96,256]{2,1,0:T(8,128)(2,1)S(1)} %copy-done.15), channel_id=1, source_target_pairs={{0,1},{1,2},{2,3},{3,0},{4,5},{5,6},{6,7},{7,4},{8,9},{9,10},{10,1... | collective-permute-start | bytes 442376 | tf_op jit(solution)/shard_map/ppermute | solution.py:627
  359.5 24.8 %collective-permute-start.4 = (bf16[9,96,256]{2,1,0:T(8,128)(2,1)S(1)}, bf16[9,96,256]{2,1,0:T(8,128)(2,1)S(1)}, u32[]{:S(2)}, u32[]{:S(2)}) collective-permute-start(bf16[9,96,256]{2,1,0:T(8,128)(2,1)S(1)} %collective-permute-done.1.refs_3_), channel_id=1, source_target_pairs={{0,3},{1,0},{2,1},{3,2},{4,7},{5,4},{6,5},{7,6},{8,11},{9,8},{10,9... | collective-permute-start | bytes 1327112 | tf_op jit(solution)/shard_map/ppermute | solution.py:627
  360.0 24.3 %collective-permute-start.3 = (bf16[9,96,256]{2,1,0:T(8,128)(2,1)S(1)}, bf16[9,96,256]{2,1,0:T(8,128)(2,1)S(1)}, u32[]{:S(2)}, u32[]{:S(2)}) collective-permute-start(bf16[9,96,256]{2,1,0:T(8,128)(2,1)S(1)} %collective-permute-done.2.refs_6_), channel_id=1, source_target_pairs={{0,1},{1,2},{2,3},{3,0},{4,5},{5,6},{6,7},{7,4},{8,9},{9,10},{10,1... | collective-permute-start | bytes 1327112 | tf_op jit(solution)/shard_map/ppermute | solution.py:627
  384.3 0.8 copy-start.9
  384.3 0.9 copy-start.10
  384.3 1.0 copy-start.11
  384.3 1.1 copy-start.12
